TPU v7x, 8 devices: a whole 2x2x1 slice. The times are simulated.
8 devices in a mesh: dp: 2 (over z, y), tp: 4 (over x, core).
Axes of the slice: x: 2, y: 2, z: 1, core: 2. Of those that a mesh axis runs over, the one named last changes fastest.
Arguments:
- x_steps: bfloat16 [3, 128, 6144], P(None, 'dp'), parts along dimension 1
- seq_lens: int32 [128], P(('dp', 'tp')), parts along dimension 0
- k_cache: bfloat16 [128, 2048, 128], P(('dp', 'tp')), parts along dimension 0
- v_cache: bfloat16 [128, 2048, 128], P(('dp', 'tp')), parts along dimension 0
- ln_gain: bfloat16 [6144], replicated
- ln_bias: bfloat16 [6144], replicated
- w_q: bfloat16 [6144, 6144], P(None, 'tp')
- b_q: bfloat16 [6144], P('tp')
- w_kv: bfloat16 [6144, 256], replicated
- b_kv: bfloat16 [256], replicated
- w_out: bfloat16 [6144, 6144], P('tp')
- b_out: bfloat16 [6144], replicated
Outputs:
- output 1: bfloat16 [3, 128, 6144], P(None, 'dp'), parts along dimension 1
- output 2: bfloat16 [128, 2048, 128], P(('dp', 'tp')), parts along dimension 0
- output 3: bfloat16 [128, 2048, 128], P(('dp', 'tp')), parts along dimension 0
There are 2 independent parts. A program takes and returns all parts, laid end to end along the dimension named above; an argument that names none is the same for every part.
All inputs are finite; a program needn't handle non-finite values.
Results may differ from a plain program's by a relative error of at most 0.00870897.
Values are sent between devices in bfloat16 or wider.
A program may use at most 1 GiB of HBM per device.

v0:
```python
import functools

import jax
import jax.numpy as jnp
from jax import lax
from jax.experimental import pallas as pl
from jax.experimental.pallas import tpu as pltpu
from jax.sharding import PartitionSpec as P

LN_EPS = 1e-5
LOG2E = 1.4426950408889634
MESH = pl.DeviceIdType.MESH
VMEM = pltpu.VMEM
F32 = jnp.float32
BF16 = jnp.bfloat16
LANES = 128


def send(src, dst, send_sem, recv_sem, target):
    return pltpu.make_async_remote_copy(
        src_ref=src, dst_ref=dst, send_sem=send_sem, recv_sem=recv_sem,
        device_id={"tp": target}, device_id_type=MESH,
    )


def greet(me, tp_size):
    barrier = pltpu.get_barrier_semaphore()
    for shift in range(1, tp_size):
        pl.semaphore_signal(barrier, inc=1, device_id={"tp": lax.rem(me + shift, tp_size)}, device_id_type=MESH)
    return barrier


def project_kernel(dims, x_hbm, gain_hbm, bias_hbm, wq_hbm, bq_hbm, wkv_hbm, bkv_hbm, k_hbm, v_hbm,
                   q_ref, kv_ref, k_buf, v_buf,
                   x_buf, normed, wq_buf, wkv_buf, q_send, x_sem, wq_sem, wkv_sem, send_sem, recv_sem, cache_sem,
                   gain_ref, bias_ref, bq_ref, bkv_ref, vec_sem):
    n_steps, group_rows, tp_size, n_chunks = dims
    local_rows = group_rows // tp_size
    d_model = x_buf.shape[1]
    width = wq_buf.shape[2]
    me = lax.axis_index("tp")
    x_copies = []
    for step in range(n_steps):
        rows = pl.ds(step * group_rows, group_rows)
        x_copies.append(pltpu.make_async_copy(x_hbm.at[rows], x_buf.at[rows], x_sem.at[step]))
        x_copies[-1].start()
    vectors = ((gain_hbm, gain_ref), (bias_hbm, bias_ref), (bq_hbm, bq_ref), (bkv_hbm, bkv_ref))
    vec_copies = [pltpu.make_async_copy(src, dst, vec_sem.at[idx]) for idx, (src, dst) in enumerate(vectors)]
    for copy in vec_copies:
        copy.start()

    def wq_copy(chunk):
        return pltpu.make_async_copy(wq_hbm.at[:, pl.ds(chunk * width, width)], wq_buf.at[chunk], wq_sem.at[chunk])

    wq_copy(0).start()
    wkv_copy = pltpu.make_async_copy(wkv_hbm, wkv_buf, wkv_sem)
    cache_copies = [pltpu.make_async_copy(src, dst, cache_sem.at[idx]) for idx, (src, dst) in enumerate(((k_hbm, k_buf), (v_hbm, v_buf)))]
    barrier = greet(me, tp_size)
    for copy in vec_copies:
        copy.wait()

    block = 32
    n_tiles = d_model // LANES

    def norm_block(block_idx, carry):
        rows = pl.ds(pl.multiple_of(block_idx * block, block), block)

        def tile(idx):
            return x_buf[rows, idx * LANES:(idx + 1) * LANES].astype(F32)

        total = tile(0)
        for idx in range(1, n_tiles):
            total = total + tile(idx)
        mean = jnp.sum(total, axis=1, keepdims=True) / d_model
        square = jnp.zeros((block, LANES), F32)
        for idx in range(n_tiles):
            centered = tile(idx) - mean
            square = square + centered * centered
        scale = lax.rsqrt(jnp.sum(square, axis=1, keepdims=True) / d_model + LN_EPS)
        for idx in range(n_tiles):
            lanes = slice(idx * LANES, (idx + 1) * LANES)
            out = (tile(idx) - mean) * scale * gain_ref[lanes].astype(F32)[None] + bias_ref[lanes].astype(F32)[None]
            normed[rows, lanes] = out.astype(BF16)
        return carry

    per_step = group_rows // block
    for step in range(n_steps):
        x_copies[step].wait()
        if step == n_steps - 1:
            for chunk in range(1, n_chunks):
                wq_copy(chunk).start()
        lax.fori_loop(step * per_step, (step + 1) * per_step, norm_block, 0)

    pl.semaphore_wait(barrier, tp_size - 1)

    def q_copy(chunk, shift, origin):
        target = lax.rem(origin + shift, tp_size)
        cols = pl.ds(pl.multiple_of(chunk * width, LANES), width)
        return send(
            q_send.at[:, pl.ds(pl.multiple_of(target * local_rows, local_rows), local_rows), cols],
            q_ref.at[origin, :, :, cols],
            send_sem.at[chunk, shift - 1], recv_sem.at[chunk, shift - 1], target)

    def q_chunk(chunk, carry):
        wq_copy(chunk).wait()

        @pl.when(chunk == n_chunks - 1)
        def _():
            wkv_copy.start()
            for copy in cache_copies:
                copy.start()

        cols = pl.ds(pl.multiple_of(chunk * width, LANES), width)
        part = jnp.dot(normed[...], wq_buf[chunk], preferred_element_type=F32) + bq_ref[cols].astype(F32)[None]
        q_send[:, :, cols] = part.astype(BF16).reshape(n_steps, group_rows, width)
        for shift in (2, 3, 1):
            q_copy(chunk, shift, me).start()
        own = pl.ds(pl.multiple_of(me * local_rows, local_rows), local_rows)
        q_ref[me, :, :, cols] = q_send[:, own, cols]
        return carry

    lax.fori_loop(0, n_chunks, q_chunk, 0)

    wkv_copy.wait()
    own_rows = [normed[pl.ds(pl.multiple_of(step * group_rows + me * local_rows, local_rows), local_rows), :] for step in range(n_steps)]
    own_normed = jnp.concatenate(own_rows, axis=0)
    kv_rows = jnp.dot(own_normed, wkv_buf[...], preferred_element_type=F32) + bkv_ref[...].astype(F32)[None]
    kv_rows = kv_rows.astype(BF16).astype(F32)
    head_dim = kv_ref.shape[2]
    kv_ref[0] = kv_rows[:, :head_dim]
    kv_ref[1] = kv_rows[:, head_dim:]

    for chunk in range(n_chunks):
        for shift in range(1, tp_size):
            q_copy(chunk, shift, me).wait_send()
            q_copy(chunk, shift, lax.rem(me - shift + tp_size, tp_size)).wait_recv()
    for copy in cache_copies:
        copy.wait()


def attend_kernel(lens_ref, q_ref, kv_ref, k_in, v_in,
                  a_ref, k_buf, v_buf, k_out, v_out,
                  q_rows, o_rows, scores_a, scores_b, max_a, max_b, out_sem):
    del k_in, v_in
    n_seqs, cache_len, head_dim = k_buf.shape
    n_src, n_steps, _, src_width = q_ref.shape
    src_heads = src_width // head_dim
    n_heads = n_src * src_heads
    n_rows = n_steps * n_heads
    scale = head_dim ** -0.5 * LOG2E
    key_block = 256
    n_blocks = cache_len // key_block

    def store(buf_idx, seq):
        src, dst = ((k_buf, k_out), (v_buf, v_out))[buf_idx]
        return pltpu.make_async_copy(src.at[seq], dst.at[seq], out_sem.at[buf_idx, seq])

    for src in range(n_src):
        for step in range(n_steps):
            for head in range(src_heads):
                row = (step * n_heads + src * src_heads + head) * n_seqs
                q_rows[row:row + n_seqs, :] = q_ref[src, step, :, head * head_dim:(head + 1) * head_dim].astype(F32)

    def score_stage(seq, scores, max_ref):
        length = lens_ref[seq]
        base = pl.multiple_of(jnp.minimum((length >> 4) << 4, cache_len - 32), 16)
        window = pl.ds(base, 32)
        positions = lax.broadcasted_iota(jnp.int32, (32, head_dim), 0) + base
        for buf_idx, buf in enumerate((k_buf, v_buf)):
            rows = buf[seq, window, :].astype(F32)
            for step in range(n_steps):
                fresh = kv_ref[buf_idx, pl.ds(step * n_seqs + seq, 1), :]
                rows = jnp.where(positions == length + step, fresh, rows)
            buf[seq, window, :] = rows.astype(BF16)
        queries = q_rows[pl.ds(seq, n_rows, stride=n_seqs), :].astype(BF16)
        lane = lax.broadcasted_iota(jnp.int32, (n_heads, key_block), 1)
        best = jnp.full((n_rows, LANES), -jnp.inf, F32)
        for block in range(n_blocks):
            keys = k_buf[seq, block * key_block:(block + 1) * key_block, :]
            part = lax.dot_general(queries, keys, (((1,), (1,)), ((), ())), preferred_element_type=F32)
            masked = []
            for step in range(n_steps):
                rows = part[step * n_heads:(step + 1) * n_heads, :]
                masked.append(jnp.where(lane <= length + (step - block * key_block), rows, -jnp.inf))
            part = jnp.concatenate(masked, axis=0)
            scores[:, block * key_block:(block + 1) * key_block] = part
            for idx in range(key_block // LANES):
                best = jnp.maximum(best, part[:, idx * LANES:(idx + 1) * LANES])
        max_ref[...] = jnp.broadcast_to(jnp.max(best, axis=1, keepdims=True) * scale, (n_rows, LANES))

    def value_stage(seq, scores, max_ref):
        top = max_ref[...]
        denom = jnp.zeros((n_rows, LANES), F32)
        numer = jnp.zeros((n_rows, head_dim), F32)
        for block in range(n_blocks):
            parts = []
            for idx in range(key_block // LANES):
                start = block * key_block + idx * LANES
                weight = jnp.exp2(scores[:, start:start + LANES] * scale - top)
                denom = denom + weight
                parts.append(weight.astype(BF16))
            values = v_buf[seq, block * key_block:(block + 1) * key_block, :]
            numer = numer + jnp.dot(jnp.concatenate(parts, axis=1), values, preferred_element_type=F32)
        o_rows[pl.ds(seq, n_rows, stride=n_seqs), :] = numer / jnp.sum(denom, axis=1, keepdims=True)
        store(0, seq).start()
        store(1, seq).start()

    score_stage(0, scores_a, max_a)

    def pair(idx, carry):
        seq = idx * 2
        score_stage(seq + 1, scores_b, max_b)
        value_stage(seq, scores_a, max_a)
        score_stage(seq + 2, scores_a, max_a)
        value_stage(seq + 1, scores_b, max_b)
        return carry

    lax.fori_loop(0, n_seqs // 2 - 1, pair, 0)
    score_stage(n_seqs - 1, scores_b, max_b)
    value_stage(n_seqs - 2, scores_a, max_a)
    value_stage(n_seqs - 1, scores_b, max_b)

    for step in range(n_steps):
        for head in range(n_heads):
            row = (step * n_heads + head) * n_seqs
            a_ref[step, :, head * head_dim:(head + 1) * head_dim] = o_rows[row:row + n_seqs, :].astype(BF16)

    for seq in range(n_seqs):
        store(0, seq).wait()
        store(1, seq).wait()


def emit_kernel(y_held, y_out, sem):
    copy = pltpu.make_async_copy(y_held, y_out, sem)
    copy.start()
    copy.wait()


def output_kernel(dims, a_ref, x_hbm, wo_hbm, bo_hbm,
                  y_ref,
                  x_buf, bo_ref, a_recv, wo_buf, pair_send, pair_recv, own_part, chip_sum, chip_recv,
                  x_sem, bo_sem, wo_sem, a_send_sem, a_recv_sem, pair_send_sem, pair_recv_sem,
                  chip_send_sem, chip_recv_sem, y_send_sem, y_recv_sem):
    tp_size, n_chunks, lag = dims
    n_steps, local_rows, _ = a_ref.shape
    depth = wo_buf.shape[1]
    width = wo_buf.shape[2]
    half_cols = n_chunks * width
    chip_rows = 2 * local_rows
    me = lax.axis_index("tp")
    chip, core = me // 2, lax.rem(me, 2)
    partner = chip * 2 + (1 - core)
    across = (1 - chip) * 2 + core
    barrier = greet(me, tp_size)
    bo_copy = pltpu.make_async_copy(bo_hbm, bo_ref, bo_sem)
    bo_copy.start()

    def wo_copy(chunk):
        cols = pl.ds(pl.multiple_of(chunk * width, LANES), width)
        return pltpu.make_async_copy(wo_hbm.at[:, cols], wo_buf.at[chunk], wo_sem.at[chunk])

    for idx in range(n_chunks):
        wo_copy((1 - core) * n_chunks + idx).start()
        wo_copy(core * n_chunks + idx).start()
    x_copy = pltpu.make_async_copy(x_hbm, x_buf, x_sem)
    x_copy.start()

    def a_copy(shift, origin):
        target = lax.rem(origin + shift, tp_size)
        return send(
            a_ref.at[:, :, pl.ds(pl.multiple_of(target * depth, LANES), depth)],
            a_recv.at[:, pl.ds(pl.multiple_of(origin * local_rows, local_rows), local_rows), :],
            a_send_sem.at[shift - 1], a_recv_sem.at[shift - 1], target)

    pl.semaphore_wait(barrier, tp_size - 1)
    for shift in (2, 3, 1):
        a_copy(shift, me).start()
    own = pl.ds(pl.multiple_of(me * local_rows, local_rows), local_rows)
    a_recv[:, own, :] = a_ref[:, :, pl.ds(pl.multiple_of(me * depth, LANES), depth)]

    def a_wait(origin):
        shift = lax.rem(me - origin + tp_size, tp_size)
        send(a_ref.at[:, :, pl.ds(0, depth)],
             a_recv.at[:, pl.ds(pl.multiple_of(origin * local_rows, local_rows), local_rows), :],
             a_send_sem.at[0], a_recv_sem.at[shift - 1], me).wait_recv()

    def pair_copy(unit):
        return send(pair_send.at[unit], pair_recv.at[unit], pair_send_sem.at[unit], pair_recv_sem.at[unit], partner)

    def chip_copy(unit):
        return send(chip_sum.at[unit], chip_recv.at[unit], chip_send_sem.at[unit], chip_recv_sem.at[unit], across)

    def multiply(group, chunk):
        unit = group * n_chunks + chunk
        rows_of = chip if group == 0 else 1 - chip
        rows = pl.ds(pl.multiple_of(rows_of * chip_rows, chip_rows), chip_rows)
        lhs = a_recv[:, rows, :].reshape(n_steps * chip_rows, depth)
        theirs, mine = (1 - core) * n_chunks + chunk, core * n_chunks + chunk
        if group == 0:
            wo_copy(theirs).wait()
        part = jnp.dot(lhs, wo_buf[theirs], preferred_element_type=F32)
        pair_send[unit] = part.astype(BF16).reshape(n_steps, chip_rows, width)
        pair_copy(unit).start()
        if group == 0:
            wo_copy(mine).wait()
        part = jnp.dot(lhs, wo_buf[mine], preferred_element_type=F32)
        own_part[unit] = part.reshape(n_steps, chip_rows, width)

    def reduce(unit):
        pair_copy(unit).wait_recv()
        chip_sum[unit] = (own_part[unit] + pair_recv[unit].astype(F32)).astype(BF16)
        chip_copy(unit).start()

    def first(chunk, carry):
        multiply(0, chunk)

        @pl.when(chunk >= lag)
        def _():
            reduce(chunk - lag)
        return carry

    def second(chunk, carry):
        multiply(1, chunk)
        reduce(n_chunks + chunk - lag)
        return carry

    a_wait(partner)
    lax.fori_loop(0, n_chunks, first, 0)
    a_wait(across)
    a_wait((1 - chip) * 2 + (1 - core))
    lax.fori_loop(0, n_chunks, second, 0)
    for idx in range(lag):
        reduce(2 * n_chunks - lag + idx)

    x_copy.wait()
    bo_copy.wait()

    def y_copy(unit, core_of):
        group = unit // n_chunks
        chunk = lax.rem(unit, n_chunks)
        rows_of = jnp.where(group == 0, 1 - chip, chip)
        rows = pl.ds(pl.multiple_of(rows_of * chip_rows, chip_rows), chip_rows)
        cols = pl.ds(pl.multiple_of(core_of * half_cols + chunk * width, LANES), width)
        return send(y_ref.at[:, rows, cols], y_ref.at[:, rows, cols], y_send_sem.at[unit], y_recv_sem.at[unit], partner)

    def finish(group):
        rows_of = (1 - chip) if group == 0 else chip
        rows = pl.ds(pl.multiple_of(rows_of * chip_rows, chip_rows), chip_rows)

        def body(chunk, carry):
            unit = group * n_chunks + chunk
            mine = (1 - group) * n_chunks + chunk
            cols = pl.ds(pl.multiple_of(core * half_cols + chunk * width, LANES), width)
            chip_copy(unit).wait_recv()
            total = chip_sum[mine].astype(F32) + chip_recv[unit].astype(F32)
            out = x_buf[:, rows, cols].astype(F32) + total + bo_ref[cols].astype(F32)[None, None]
            y_ref[:, rows, cols] = out.astype(BF16)
            y_copy(unit, core).start()
            return carry
        return body

    lax.fori_loop(0, n_chunks, finish(0), 0)
    lax.fori_loop(0, n_chunks, finish(1), 0)

    def drain(unit, carry):
        pair_copy(unit).wait_send()
        chip_copy(unit).wait_send()
        y_copy(unit, core).wait_send()
        y_copy(unit, 1 - core).wait_recv()
        return carry

    lax.fori_loop(0, 2 * n_chunks, drain, 0)
    for shift in range(1, tp_size):
        a_copy(shift, me).wait_send()


def in_hbm(array):
    return pltpu.with_memory_space_constraint(array, pltpu.HBM)


def spec(space):
    return pl.BlockSpec(memory_space=space)


def solution(mesh):
    tp_size = mesh.shape["tp"]

    def local_block(x_steps, seq_lens, k_cache, v_cache, ln_gain, ln_bias, w_q, b_q, w_kv, b_kv, w_out, b_out):
        n_steps, group_rows, d_model = x_steps.shape
        local_rows, cache_len, head_dim = k_cache.shape
        q_cols = w_q.shape[1]
        n_heads = q_cols * tp_size // head_dim
        limit = 34 * 2 ** 20
        dma = pltpu.SemaphoreType.DMA

        q_chunks = 3
        q_blocks, kv_rows, k_held, v_held = pl.pallas_call(
            functools.partial(project_kernel, (n_steps, group_rows, tp_size, q_chunks)),
            out_shape=(
                VMEM((tp_size, n_steps, local_rows, q_cols), BF16),
                VMEM((2, n_steps * local_rows, head_dim), F32),
                VMEM(k_cache.shape, BF16),
                VMEM(v_cache.shape, BF16),
            ),
            in_specs=[spec(pl.ANY)] * 9,
            out_specs=(spec(VMEM),) * 4,
            scratch_shapes=[
                VMEM((n_steps * group_rows, d_model), BF16),
                VMEM((n_steps * group_rows, d_model), BF16),
                VMEM((q_chunks, d_model, q_cols // q_chunks), BF16),
                VMEM((d_model, 2 * head_dim), BF16),
                VMEM((n_steps, group_rows, q_cols), BF16),
                dma((n_steps,)), dma((q_chunks,)), dma,
                dma((q_chunks, tp_size - 1)), dma((q_chunks, tp_size - 1)), dma((2,)),
                VMEM(ln_gain.shape, BF16), VMEM(ln_bias.shape, BF16), VMEM(b_q.shape, BF16), VMEM(b_kv.shape, BF16), dma((4,)),
            ],
            compiler_params=pltpu.CompilerParams(collective_id=0, has_side_effects=True, vmem_limit_bytes=limit),
            name="project",
        )(*(in_hbm(arg) for arg in (x_steps.reshape(n_steps * group_rows, d_model), ln_gain, ln_bias, w_q, b_q, w_kv, b_kv, k_cache, v_cache)))

        n_rows = n_steps * n_heads
        attn, _, _, k_new, v_new = pl.pallas_call(
            attend_kernel,
            out_shape=(
                VMEM((n_steps, local_rows, n_heads * head_dim), BF16),
                VMEM(k_cache.shape, BF16),
                VMEM(v_cache.shape, BF16),
                jax.ShapeDtypeStruct(k_cache.shape, BF16),
                jax.ShapeDtypeStruct(v_cache.shape, BF16),
            ),
            in_specs=[spec(pltpu.SMEM)] + [spec(VMEM)] * 4,
            out_specs=(spec(VMEM),) * 3 + (spec(pl.ANY),) * 2,
            input_output_aliases={3: 1, 4: 2},
            scratch_shapes=[
                VMEM((n_rows * local_rows, head_dim), F32),
                VMEM((n_rows * local_rows, head_dim), F32),
                VMEM((n_rows, cache_len), F32),
                VMEM((n_rows, cache_len), F32),
                VMEM((n_rows, LANES), F32),
                VMEM((n_rows, LANES), F32),
                dma((2, local_rows)),
            ],
            compiler_params=pltpu.CompilerParams(vmem_limit_bytes=12 * 2 ** 20),
            name="attend",
        )(seq_lens, q_blocks, kv_rows, k_held, v_held)

        o_chunks = 6
        width = d_model // (2 * o_chunks)
        units = (2 * o_chunks, n_steps, 2 * local_rows, width)
        y_held = pl.pallas_call(
            functools.partial(output_kernel, (tp_size, o_chunks, 3)),
            out_shape=VMEM(x_steps.shape, BF16),
            in_specs=[spec(VMEM), spec(pl.ANY), spec(pl.ANY), spec(pl.ANY)],
            out_specs=spec(VMEM),
            scratch_shapes=[
                VMEM(x_steps.shape, BF16), VMEM(b_out.shape, BF16),
                VMEM((n_steps, group_rows, q_cols), BF16),
                VMEM((2 * o_chunks, q_cols, width), BF16),
                VMEM(units, BF16), VMEM(units, BF16), VMEM(units, F32), VMEM(units, BF16), VMEM(units, BF16),
                dma, dma, dma((2 * o_chunks,)), dma((tp_size - 1,)), dma((tp_size - 1,)),
                dma((2 * o_chunks,)), dma((2 * o_chunks,)), dma((2 * o_chunks,)),
                dma((2 * o_chunks,)), dma((2 * o_chunks,)), dma((2 * o_chunks,)),
            ],
            compiler_params=pltpu.CompilerParams(collective_id=1, has_side_effects=True, vmem_limit_bytes=limit),
            name="output",
        )(attn, in_hbm(x_steps), in_hbm(w_out), in_hbm(b_out))
        y_steps = pl.pallas_call(
            emit_kernel,
            out_shape=jax.ShapeDtypeStruct(x_steps.shape, BF16),
            in_specs=[spec(VMEM)],
            out_specs=spec(pl.ANY),
            scratch_shapes=[dma],
            compiler_params=pltpu.CompilerParams(vmem_limit_bytes=2 ** 20),
            name="emit",
        )(y_held)
        return y_steps, k_new, v_new

    row_spec = P(('dp', 'tp'), None, None)
    return jax.shard_map(
        local_block,
        mesh=mesh,
        in_specs=(P(None, 'dp', None), P(('dp', 'tp')), row_spec, row_spec, P(None), P(None), P(None, 'tp'), P('tp'), P(None, None), P(None), P('tp', None), P(None)),
        out_specs=(P(None, 'dp', None), row_spec, row_spec),
        check_vma=False,
    )
```

profile of v0, /device:TPU:0, one launch (start us, length us, event | category | flops | bytes accessed | tf_op | source)
XLA Modules:
  0.0 66.0 jit_solution(8441145943872470275)
XLA Ops:
  0.6 0.0 copy-start
  0.6 15.7 %project.1 = (bf16[4,3,16,1536]{3,2,1,0:T(8,128)(2,1)S(1)}, f32[2,48,128]{2,1,0:T(8,128)S(1)}, bf16[16,2048,128]{2,1,0:T(8,128)(2,1)S(1)}, bf16[16,2048,128]{2,1,0:T(8,128)(2,1)S(1)}) custom-call(bf16[192,6144]{1,0:T(8,128)(2,1)} %bitcast.1, bf16[6144]{0:T(1024)(128)(2,1)} %gain_hbm.1, bf16[6144]{0:T(1024)(128)(2,1)} %bias_hbm.1, bf16[6144,1536]{1,0:T(8,128)(2,1)} %wq_hbm.1, ...), custom_call_target="tpu_custom_call" | custom-call | tf_op jit(solution)/shard_map/project/pallas_call | solution.py:397
  16.3 0.0 copy-done
  16.4 10.9 %attend.1 = (bf16[3,16,6144]{2,1,0:T(8,128)(2,1)S(1)}, bf16[16,2048,128]{2,1,0:T(8,128)(2,1)S(1)}, bf16[16,2048,128]{2,1,0:T(8,128)(2,1)S(1)}, bf16[16,2048,128]{2,1,0:T(8,128)(2,1)}, bf16[16,2048,128]{2,1,0:T(8,128)(2,1)}) custom-call(s32[16]{0:T(128)S(1)} %copy-done, ...), custom_call_target="tpu_custom_call", output_to_operand_aliasing={{1}: (3, {}), {2}: (4, {})} | custom-call | tf_op jit(solution)/shard_map/attend/pallas_call | solution.py:422
  27.2 37.3 %output.1.y_held = bf16[3,64,6144]{2,1,0:T(8,128)(2,1)S(1)} custom-call(bf16[3,16,6144]{2,1,0:T(8,128)(2,1)S(1)} %get-tuple-element.14.a_ref, bf16[3,64,6144]{2,1,0:T(8,128)(2,1)} %x_hbm.1, bf16[1536,6144]{1,0:T(8,128)(2,1)} %wo_hbm.1, bf16[6144]{0:T(1024)(128)(2,1)} %bo_hbm.1), custom_call_target="tpu_custom_call" | custom-call | tf_op jit(solution)/shard_map/output/pallas_call | solution.py:450
  64.5 1.4 %emit.1 = bf16[3,64,6144]{2,1,0:T(8,128)(2,1)} custom-call(bf16[3,64,6144]{2,1,0:T(8,128)(2,1)S(1)} %output.1.y_held), custom_call_target="tpu_custom_call" | custom-call | tf_op jit(solution)/shard_map/emit/pallas_call | solution.py:467
Async XLA Ops:
  0.6 15.7 %copy-start = (s32[16]{0:T(128)S(1)}, s32[16]{0:T(128)}, u32[]{:S(2)}) copy-start(s32[16]{0:T(128)} %lens_ref.1) | copy-start | bytes 196
where the time goes:
time: 66.1 us; the launch traced here: 66 us
  Pallas kernels  65.3 us (99%)
  between operations  0.67 us (1%)
    pallas_call x1, Pallas kernels, local_block(): pl.pallas_call(functools.partial(output_kernel, (tp_size, o_chunks, 3)),...  37.3 us
    pallas_call x1, Pallas kernels, local_block(): pl.pallas_call(functools.partial(project_kernel, (n_steps, group_rows, tp...  15.7 us
    pallas_call x1, Pallas kernels, local_block(): pl.pallas_call(attend_kernel, out_shape=(VMEM((n_steps, local_rows, n_hea...  10.9 us
    pallas_call x1, Pallas kernels, local_block(): pl.pallas_call(emit_kernel, out_shape=jax.ShapeDtypeStruct(x_steps.shape,...  1.42 us

commit v1 on v0

v1 whole, which is shorter than its diff:
```python
import functools

import jax
import jax.numpy as jnp
from jax import lax
from jax.experimental import pallas as pl
from jax.experimental.pallas import tpu as pltpu
from jax.sharding import PartitionSpec as P

LN_EPS = 1e-5
LOG2E = 1.4426950408889634
MESH = pl.DeviceIdType.MESH
VMEM = pltpu.VMEM
F32 = jnp.float32
BF16 = jnp.bfloat16
LANES = 128


def send(src, dst, send_sem, recv_sem, target):
    return pltpu.make_async_remote_copy(
        src_ref=src, dst_ref=dst, send_sem=send_sem, recv_sem=recv_sem,
        device_id={"tp": target}, device_id_type=MESH,
    )


def greet(me, tp_size):
    barrier = pltpu.get_barrier_semaphore()
    for shift in range(1, tp_size):
        pl.semaphore_signal(barrier, inc=1, device_id={"tp": lax.rem(me + shift, tp_size)}, device_id_type=MESH)
    return barrier


def project_kernel(dims, x_hbm, gain_hbm, bias_hbm, wq_hbm, bq_hbm, wkv_hbm, bkv_hbm, k_hbm, v_hbm,
                   q_ref, kv_ref, k_buf, v_buf,
                   x_buf, normed, wq_buf, wkv_buf, q_send, gain_ref, bias_ref, bq_ref, bkv_ref,
                   x_sem, wq_sem, wkv_sem, cache_sem, vec_sem, send_sem, recv_sem):
    n_steps, group_rows, tp_size, n_chunks, block = dims
    local_rows = group_rows // tp_size
    n_rows, d_model = x_buf.shape
    n_blocks = n_rows // block
    n_tiles = d_model // LANES
    width = wq_buf.shape[2]
    first_chunks = n_chunks // 2
    me = lax.axis_index("tp")

    def x_copy(idx):
        rows = pl.ds(pl.multiple_of(idx * block, block), block)
        return pltpu.make_async_copy(x_hbm.at[rows], x_buf.at[rows], x_sem.at[idx])

    def wq_copy(chunk):
        cols = pl.ds(pl.multiple_of(chunk * width, LANES), width)
        return pltpu.make_async_copy(wq_hbm.at[:, cols], wq_buf.at[chunk], wq_sem.at[chunk])

    for idx in range(n_blocks):
        x_copy(idx).start()
    vectors = ((gain_hbm, gain_ref), (bias_hbm, bias_ref), (bq_hbm, bq_ref), (bkv_hbm, bkv_ref))
    vec_copies = [pltpu.make_async_copy(src, dst, vec_sem.at[idx]) for idx, (src, dst) in enumerate(vectors)]
    for copy in vec_copies:
        copy.start()
    late_copies = [pltpu.make_async_copy(wkv_hbm, wkv_buf, wkv_sem)]
    for idx, (src, dst) in enumerate(((k_hbm, k_buf), (v_hbm, v_buf))):
        late_copies.append(pltpu.make_async_copy(src, dst, cache_sem.at[idx]))
    barrier = greet(me, tp_size)
    for copy in vec_copies:
        copy.wait()

    def norm_block(idx, carry):
        x_copy(idx).wait()

        @pl.when(idx == 0)
        def _():
            for chunk in range(first_chunks):
                wq_copy(chunk).start()

        rows = pl.ds(pl.multiple_of(idx * block, block), block)

        def tile(col):
            return x_buf[rows, col * LANES:(col + 1) * LANES].astype(F32)

        total = tile(0)
        for col in range(1, n_tiles):
            total = total + tile(col)
        mean = jnp.sum(total, axis=1, keepdims=True) / d_model
        square = jnp.zeros((block, LANES), F32)
        for col in range(n_tiles):
            centered = tile(col) - mean
            square = square + centered * centered
        scale = lax.rsqrt(jnp.sum(square, axis=1, keepdims=True) / d_model + LN_EPS)
        for col in range(n_tiles):
            lanes = slice(col * LANES, (col + 1) * LANES)
            out = (tile(col) - mean) * scale * gain_ref[lanes].astype(F32)[None] + bias_ref[lanes].astype(F32)[None]
            normed[rows, lanes] = out.astype(BF16)
        return carry

    lax.fori_loop(0, n_blocks, norm_block, 0)
    for chunk in range(first_chunks, n_chunks):
        wq_copy(chunk).start()
    pl.semaphore_wait(barrier, tp_size - 1)

    def q_copy(chunk, shift, origin):
        target = lax.rem(origin + shift, tp_size)
        cols = pl.ds(pl.multiple_of(chunk * width, LANES), width)
        return send(
            q_send.at[:, pl.ds(pl.multiple_of(target * local_rows, local_rows), local_rows), cols],
            q_ref.at[origin, :, :, cols],
            send_sem.at[chunk, shift - 1], recv_sem.at[chunk, shift - 1], target)

    def q_chunk(chunk, carry):
        wq_copy(chunk).wait()

        @pl.when(chunk == first_chunks)
        def _():
            for copy in late_copies:
                copy.start()

        cols = pl.ds(pl.multiple_of(chunk * width, LANES), width)
        part = jnp.dot(normed[...], wq_buf[chunk], preferred_element_type=F32) + bq_ref[cols].astype(F32)[None]
        q_send[:, :, cols] = part.astype(BF16).reshape(n_steps, group_rows, width)
        for shift in (2, 3, 1):
            q_copy(chunk, shift, me).start()
        own = pl.ds(pl.multiple_of(me * local_rows, local_rows), local_rows)
        q_ref[me, :, :, cols] = q_send[:, own, cols]
        return carry

    lax.fori_loop(0, n_chunks, q_chunk, 0)

    late_copies[0].wait()
    own_rows = [normed[pl.ds(pl.multiple_of(step * group_rows + me * local_rows, local_rows), local_rows), :] for step in range(n_steps)]
    own_normed = jnp.concatenate(own_rows, axis=0)
    kv_rows = jnp.dot(own_normed, wkv_buf[...], preferred_element_type=F32) + bkv_ref[...].astype(F32)[None]
    kv_rows = kv_rows.astype(BF16).astype(F32)
    head_dim = kv_ref.shape[2]
    kv_ref[0] = kv_rows[:, :head_dim]
    kv_ref[1] = kv_rows[:, head_dim:]

    def drain(chunk, carry):
        for shift in range(1, tp_size):
            q_copy(chunk, shift, me).wait_send()
            q_copy(chunk, shift, lax.rem(me - shift + tp_size, tp_size)).wait_recv()
        return carry

    lax.fori_loop(0, n_chunks, drain, 0)
    for copy in late_copies[1:]:
        copy.wait()


def attend_set(first_seq, lens_ref, q_ref, k_buf, v_buf, a_ref, q_rows, o_rows, scores_a, scores_b, max_a, max_b):
    n_steps, n_seqs, _ = a_ref.shape
    _, cache_len, head_dim = k_buf.shape
    n_src, _, _, src_width = q_ref.shape
    src_heads = src_width // head_dim
    n_heads = n_src * src_heads
    n_rows = n_steps * n_heads
    scale = head_dim ** -0.5 * LOG2E
    key_block = 256
    n_blocks = cache_len // key_block

    for src in range(n_src):
        for step in range(n_steps):
            for head in range(src_heads):
                row = (step * n_heads + src * src_heads + head) * n_seqs
                heads = q_ref[src, step, first_seq:first_seq + n_seqs, head * head_dim:(head + 1) * head_dim]
                q_rows[row:row + n_seqs, :] = heads.astype(F32)

    def score_stage(seq, scores, max_ref):
        length = lens_ref[first_seq + seq]
        queries = q_rows[pl.ds(seq, n_rows, stride=n_seqs), :].astype(BF16)
        lane = lax.broadcasted_iota(jnp.int32, (n_heads, key_block), 1)
        best = jnp.full((n_rows, LANES), -jnp.inf, F32)
        for block in range(n_blocks):
            keys = k_buf[first_seq + seq, block * key_block:(block + 1) * key_block, :]
            part = lax.dot_general(queries, keys, (((1,), (1,)), ((), ())), preferred_element_type=F32)
            masked = []
            for step in range(n_steps):
                rows = part[step * n_heads:(step + 1) * n_heads, :]
                masked.append(jnp.where(lane <= length + (step - block * key_block), rows, -jnp.inf))
            part = jnp.concatenate(masked, axis=0)
            scores[:, block * key_block:(block + 1) * key_block] = part
            for idx in range(key_block // LANES):
                best = jnp.maximum(best, part[:, idx * LANES:(idx + 1) * LANES])
        max_ref[...] = jnp.broadcast_to(jnp.max(best, axis=1, keepdims=True) * scale, (n_rows, LANES))

    def value_stage(seq, scores, max_ref):
        top = max_ref[...]
        denom = jnp.zeros((n_rows, LANES), F32)
        numer = jnp.zeros((n_rows, head_dim), F32)
        for block in range(n_blocks):
            parts = []
            for idx in range(key_block // LANES):
                start = block * key_block + idx * LANES
                weight = jnp.exp2(scores[:, start:start + LANES] * scale - top)
                denom = denom + weight
                parts.append(weight.astype(BF16))
            values = v_buf[first_seq + seq, block * key_block:(block + 1) * key_block, :]
            numer = numer + jnp.dot(jnp.concatenate(parts, axis=1), values, preferred_element_type=F32)
        o_rows[pl.ds(seq, n_rows, stride=n_seqs), :] = numer / jnp.sum(denom, axis=1, keepdims=True)

    score_stage(0, scores_a, max_a)

    def pair(idx, carry):
        seq = idx * 2
        score_stage(seq + 1, scores_b, max_b)
        value_stage(seq, scores_a, max_a)
        score_stage(seq + 2, scores_a, max_a)
        value_stage(seq + 1, scores_b, max_b)
        return carry

    lax.fori_loop(0, n_seqs // 2 - 1, pair, 0)
    score_stage(n_seqs - 1, scores_b, max_b)
    value_stage(n_seqs - 2, scores_a, max_a)
    value_stage(n_seqs - 1, scores_b, max_b)

    for step in range(n_steps):
        for head in range(n_heads):
            row = (step * n_heads + head) * n_seqs
            a_ref[step, :, head * head_dim:(head + 1) * head_dim] = o_rows[row:row + n_seqs, :].astype(BF16)


def attend_kernel(lens_ref, q_ref, kv_ref, k_in, v_in,
                  a_ref, k_buf, v_buf, k_out, v_out,
                  q_rows, o_rows, scores_a, scores_b, max_a, max_b, out_sem):
    del k_in, v_in
    n_seqs, cache_len, head_dim = k_buf.shape
    n_steps = a_ref.shape[0]

    def store(buf_idx, seq):
        src, dst = ((k_buf, k_out), (v_buf, v_out))[buf_idx]
        return pltpu.make_async_copy(src.at[seq], dst.at[seq], out_sem.at[buf_idx, seq])

    def update(seq, carry):
        length = lens_ref[seq]
        base = pl.multiple_of(jnp.minimum((length >> 4) << 4, cache_len - 32), 16)
        window = pl.ds(base, 32)
        positions = lax.broadcasted_iota(jnp.int32, (32, head_dim), 0) + base
        for buf_idx, buf in enumerate((k_buf, v_buf)):
            rows = buf[seq, window, :].astype(F32)
            for step in range(n_steps):
                fresh = kv_ref[buf_idx, pl.ds(step * n_seqs + seq, 1), :]
                rows = jnp.where(positions == length + step, fresh, rows)
            buf[seq, window, :] = rows.astype(BF16)
        return carry

    def write(seq, carry):
        store(0, seq).start()
        store(1, seq).start()
        return carry

    def finish(seq, carry):
        store(0, seq).wait()
        store(1, seq).wait()
        return carry

    lax.fori_loop(0, n_seqs, update, 0)
    lax.fori_loop(0, n_seqs, write, 0)
    attend_set(0, lens_ref, q_ref, k_buf, v_buf, a_ref, q_rows, o_rows, scores_a, scores_b, max_a, max_b)
    lax.fori_loop(0, n_seqs, finish, 0)


def emit_kernel(y_held, y_out, sem):
    copy = pltpu.make_async_copy(y_held, y_out, sem)
    copy.start()
    copy.wait()


def output_kernel(dims, lens_ref, q_ref, k_buf, v_buf, a_first, x_hbm, wo_hbm, bo_hbm,
                  y_ref,
                  bo_ref, a_second, a_recv, wo_buf, pair_send, pair_recv, chip_sum, chip_recv,
                  q_rows, o_rows, scores_a, scores_b, max_a, max_b,
                  x_sem, bo_sem, wo_sem, a_send_sem, a_recv_sem, pair_send_sem, pair_recv_sem,
                  chip_send_sem, chip_recv_sem, y_send_sem, y_recv_sem):
    tp_size, n_chunks, lag = dims
    n_steps, set_rows, _ = a_first.shape
    depth = wo_buf.shape[1]
    width = wo_buf.shape[2]
    half_cols = n_chunks * width
    n_units = 2 * n_chunks
    me = lax.axis_index("tp")
    chip, core = me // 2, lax.rem(me, 2)
    partner = chip * 2 + (1 - core)
    across = (1 - chip) * 2 + core
    barrier = greet(me, tp_size)

    def wo_copy(chunk):
        cols = pl.ds(pl.multiple_of(chunk * width, LANES), width)
        return pltpu.make_async_copy(wo_hbm.at[:, cols], wo_buf.at[chunk], wo_sem.at[chunk])

    for idx in range(n_chunks):
        wo_copy((1 - core) * n_chunks + idx).start()
        wo_copy(core * n_chunks + idx).start()
    bo_copy = pltpu.make_async_copy(bo_hbm, bo_ref, bo_sem)
    bo_copy.start()
    half = pl.ds(pl.multiple_of(core * half_cols, LANES), half_cols)
    x_copy = pltpu.make_async_copy(x_hbm.at[:, :, :, :, half], y_ref.at[:, :, :, :, half], x_sem)
    x_copy.start()
    sets = (a_first, a_second)

    def a_copy(group, shift, origin):
        target = lax.rem(origin + shift, tp_size)
        return send(
            sets[group].at[:, :, pl.ds(pl.multiple_of(target * depth, LANES), depth)],
            a_recv.at[group, :, origin],
            a_send_sem.at[group, shift - 1], a_recv_sem.at[group, shift - 1], target)

    def exchange(group):
        for shift in (2, 3, 1):
            a_copy(group, shift, me).start()
        a_recv[group, :, me] = sets[group][:, :, pl.ds(pl.multiple_of(me * depth, LANES), depth)]

    def received(group):
        for shift in range(1, tp_size):
            a_copy(group, shift, lax.rem(me - shift + tp_size, tp_size)).wait_recv()

    def pair_copy(unit):
        return send(pair_send.at[unit], pair_recv.at[unit], pair_send_sem.at[unit], pair_recv_sem.at[unit], partner)

    def chip_copy(unit):
        return send(chip_sum.at[unit], chip_recv.at[unit], chip_send_sem.at[unit], chip_recv_sem.at[unit], across)

    def operand(group):
        return a_recv[group].reshape(n_steps * tp_size * set_rows, depth)

    def multiply(group, chunk):
        unit = group * n_chunks + chunk
        theirs = (1 - core) * n_chunks + chunk
        if group == 0:
            wo_copy(theirs).wait()
        part = jnp.dot(operand(group), wo_buf[theirs], preferred_element_type=F32)
        pair_send[unit] = part.astype(BF16)
        pair_copy(unit).start()

    def reduce(group, chunk):
        unit = group * n_chunks + chunk
        mine = core * n_chunks + chunk
        if group == 0:
            wo_copy(mine).wait()
        part = jnp.dot(operand(group), wo_buf[mine], preferred_element_type=F32)
        pair_copy(unit).wait_recv()
        chip_sum[unit] = (part + pair_recv[unit].astype(F32)).astype(BF16)
        chip_copy(unit).start()

    def project(group):
        def body(chunk, carry):
            @pl.when(chunk < n_chunks)
            def _():
                multiply(group, chunk)

            @pl.when(chunk >= lag)
            def _():
                reduce(group, chunk - lag)
            return carry

        lax.fori_loop(0, n_chunks + lag, body, 0)

    pl.semaphore_wait(barrier, tp_size - 1)
    exchange(0)
    attend_set(set_rows, lens_ref, q_ref, k_buf, v_buf, a_second, q_rows, o_rows, scores_a, scores_b, max_a, max_b)
    exchange(1)
    received(0)
    project(0)
    received(1)
    project(1)

    x_copy.wait()
    bo_copy.wait()

    def y_copy(unit, core_of):
        group = unit // n_chunks
        chunk = lax.rem(unit, n_chunks)
        cols = pl.ds(pl.multiple_of(core_of * half_cols + chunk * width, LANES), width)
        block = y_ref.at[:, :, group, :, cols]
        return send(block, block, y_send_sem.at[unit], y_recv_sem.at[unit], partner)

    def combine(group):
        def body(chunk, carry):
            unit = group * n_chunks + chunk
            cols = pl.ds(pl.multiple_of(core * half_cols + chunk * width, LANES), width)
            chip_copy(unit).wait_recv()
            total = chip_sum[unit].astype(F32) + chip_recv[unit].astype(F32)
            total = total.reshape(n_steps, tp_size, set_rows, width)
            out = y_ref[:, :, group, :, cols].astype(F32) + total + bo_ref[cols].astype(F32)[None, None, None]
            y_ref[:, :, group, :, cols] = out.astype(BF16)
            y_copy(unit, core).start()
            return carry
        return body

    lax.fori_loop(0, n_chunks, combine(0), 0)
    lax.fori_loop(0, n_chunks, combine(1), 0)

    def drain(unit, carry):
        pair_copy(unit).wait_send()
        chip_copy(unit).wait_send()
        y_copy(unit, core).wait_send()
        y_copy(unit, 1 - core).wait_recv()
        return carry

    lax.fori_loop(0, n_units, drain, 0)
    for group in range(2):
        for shift in range(1, tp_size):
            a_copy(group, shift, me).wait_send()


def in_hbm(array):
    return pltpu.with_memory_space_constraint(array, pltpu.HBM)


def spec(space):
    return pl.BlockSpec(memory_space=space)


def solution(mesh):
    tp_size = mesh.shape["tp"]

    def local_block(x_steps, seq_lens, k_cache, v_cache, ln_gain, ln_bias, w_q, b_q, w_kv, b_kv, w_out, b_out):
        n_steps, group_rows, d_model = x_steps.shape
        local_rows, cache_len, head_dim = k_cache.shape
        q_cols = w_q.shape[1]
        n_heads = q_cols * tp_size // head_dim
        n_x = n_steps * group_rows
        mib = 2 ** 20
        dma = pltpu.SemaphoreType.DMA

        q_chunks, block = 6, 32
        remote = dma((q_chunks, tp_size - 1))
        q_blocks, kv_rows, k_held, v_held = pl.pallas_call(
            functools.partial(project_kernel, (n_steps, group_rows, tp_size, q_chunks, block)),
            out_shape=(
                VMEM((tp_size, n_steps, local_rows, q_cols), BF16),
                VMEM((2, n_steps * local_rows, head_dim), F32),
                VMEM(k_cache.shape, BF16),
                VMEM(v_cache.shape, BF16),
            ),
            in_specs=[spec(pl.ANY)] * 9,
            out_specs=(spec(VMEM),) * 4,
            scratch_shapes=[
                VMEM((n_x, d_model), BF16),
                VMEM((n_x, d_model), BF16),
                VMEM((q_chunks, d_model, q_cols // q_chunks), BF16),
                VMEM((d_model, 2 * head_dim), BF16),
                VMEM((n_steps, group_rows, q_cols), BF16),
                VMEM(ln_gain.shape, BF16), VMEM(ln_bias.shape, BF16), VMEM(b_q.shape, BF16), VMEM(b_kv.shape, BF16),
                dma((n_x // block,)), dma((q_chunks,)), dma, dma((2,)), dma((4,)), remote, remote,
            ],
            compiler_params=pltpu.CompilerParams(collective_id=0, has_side_effects=True, vmem_limit_bytes=31 * mib),
            name="project",
        )(*(in_hbm(arg) for arg in (x_steps.reshape(n_x, d_model), ln_gain, ln_bias, w_q, b_q, w_kv, b_kv, k_cache, v_cache)))

        n_rows = n_steps * n_heads
        set_rows = local_rows // 2
        attend_scratch = [
            VMEM((n_rows * set_rows, head_dim), F32),
            VMEM((n_rows * set_rows, head_dim), F32),
            VMEM((n_rows, cache_len), F32),
            VMEM((n_rows, cache_len), F32),
            VMEM((n_rows, LANES), F32),
            VMEM((n_rows, LANES), F32),
        ]
        a_set = (n_steps, set_rows, n_heads * head_dim)
        a_first, k_held, v_held, k_new, v_new = pl.pallas_call(
            attend_kernel,
            out_shape=(
                VMEM(a_set, BF16),
                VMEM(k_cache.shape, BF16),
                VMEM(v_cache.shape, BF16),
                jax.ShapeDtypeStruct(k_cache.shape, BF16),
                jax.ShapeDtypeStruct(v_cache.shape, BF16),
            ),
            in_specs=[spec(pltpu.SMEM)] + [spec(VMEM)] * 4,
            out_specs=(spec(VMEM),) * 3 + (spec(pl.ANY),) * 2,
            input_output_aliases={3: 1, 4: 2},
            scratch_shapes=attend_scratch + [dma((2, local_rows))],
            compiler_params=pltpu.CompilerParams(vmem_limit_bytes=12 * mib),
            name="attend",
        )(seq_lens, q_blocks, kv_rows, k_held, v_held)

        o_chunks = 6
        n_units = 2 * o_chunks
        width = d_model // n_units
        units = (n_units, n_steps * tp_size * set_rows, width)
        split = (n_steps, tp_size, 2, set_rows, d_model)
        y_held = pl.pallas_call(
            functools.partial(output_kernel, (tp_size, o_chunks, 3)),
            out_shape=VMEM(split, BF16),
            in_specs=[spec(pltpu.SMEM)] + [spec(VMEM)] * 4 + [spec(pl.ANY)] * 3,
            out_specs=spec(VMEM),
            scratch_shapes=[
                VMEM(b_out.shape, BF16), VMEM(a_set, BF16),
                VMEM((2, n_steps, tp_size, set_rows, q_cols), BF16),
                VMEM((n_units, q_cols, width), BF16),
                VMEM(units, BF16), VMEM(units, BF16), VMEM(units, BF16), VMEM(units, BF16),
            ] + attend_scratch + [
                dma, dma, dma((n_units,)), dma((2, tp_size - 1)), dma((2, tp_size - 1)),
            ] + [dma((n_units,))] * 6,
            compiler_params=pltpu.CompilerParams(collective_id=1, has_side_effects=True, vmem_limit_bytes=31 * mib),
            name="output",
        )(seq_lens, q_blocks, k_held, v_held, a_first, in_hbm(x_steps.reshape(split)), in_hbm(w_out), in_hbm(b_out))
        y_steps = pl.pallas_call(
            emit_kernel,
            out_shape=jax.ShapeDtypeStruct(x_steps.shape, BF16),
            in_specs=[spec(VMEM)],
            out_specs=spec(pl.ANY),
            scratch_shapes=[dma],
            compiler_params=pltpu.CompilerParams(vmem_limit_bytes=mib),
            name="emit",
        )(y_held.reshape(x_steps.shape))
        return y_steps, k_new, v_new

    row_spec = P(('dp', 'tp'), None, None)
    return jax.shard_map(
        local_block,
        mesh=mesh,
        in_specs=(P(None, 'dp', None), P(('dp', 'tp')), row_spec, row_spec, P(None), P(None), P(None, 'tp'), P('tp'), P(None, None), P(None), P('tp', None), P(None)),
        out_specs=(P(None, 'dp', None), row_spec, row_spec),
        check_vma=False,
    )
```

time: 66.1 us -> 63.6 us (0.962)
  Pallas kernels: 65.3 us -> 62.8 us
    pallas_call x1, Pallas kernels: 10.9 us -> 6.87 us  [local_block(): pl.pallas_call(attend_kernel, out_shape=(VMEM(a_set, BF16), VMEM(k_cache....]
    pallas_call x1, Pallas kernels: 37.3 us -> 38.7 us  [local_block(): pl.pallas_call(functools.partial(output_kernel, (tp_size, o_chunks, 3)),...]
where the time goes in v1:
time: 63.6 us; the launch traced here: 63.4 us
  Pallas kernels  62.8 us (99%)
  between operations  0.67 us (1%)
    pallas_call x1, Pallas kernels, local_block(): pl.pallas_call(functools.partial(output_kernel, (tp_size, o_chunks, 3)),...  38.7 us
    pallas_call x1, Pallas kernels, local_block(): pl.pallas_call(functools.partial(project_kernel, (n_steps, group_rows, tp...  15.7 us
    pallas_call x1, Pallas kernels, local_block(): pl.pallas_call(attend_kernel, out_shape=(VMEM(a_set, BF16), VMEM(k_cache....  6.87 us
    pallas_call x1, Pallas kernels, local_block(): pl.pallas_call(emit_kernel, out_shape=jax.ShapeDtypeStruct(x_steps.shape,...  1.42 us

profile of v1, /device:TPU:0, one launch (start us, length us, event | category | flops | bytes accessed | tf_op | source)
XLA Modules:
  0.0 63.4 jit_solution(15892552991781281965)
XLA Ops:
  0.6 0.0 copy-start
  0.6 15.7 %project.1 = (bf16[4,3,16,1536]{3,2,1,0:T(8,128)(2,1)S(1)}, f32[2,48,128]{2,1,0:T(8,128)S(1)}, bf16[16,2048,128]{2,1,0:T(8,128)(2,1)S(1)}, bf16[16,2048,128]{2,1,0:T(8,128)(2,1)S(1)}) custom-call(bf16[192,6144]{1,0:T(8,128)(2,1)} %bitcast.4, bf16[6144]{0:T(1024)(128)(2,1)} %gain_hbm.1, bf16[6144]{0:T(1024)(128)(2,1)} %bias_hbm.1, bf16[6144,1536]{1,0:T(8,128)(2,1)} %wq_hbm.1, ...), custom_call_target="tpu_custom_call" | custom-call | tf_op jit(solution)/shard_map/project/pallas_call | solution.py:424
  16.4 0.0 copy-done
  16.4 6.9 %attend.1 = (bf16[3,8,6144]{2,1,0:T(8,128)(2,1)S(1)}, bf16[16,2048,128]{2,1,0:T(8,128)(2,1)S(1)}, bf16[16,2048,128]{2,1,0:T(8,128)(2,1)S(1)}, bf16[16,2048,128]{2,1,0:T(8,128)(2,1)}, bf16[16,2048,128]{2,1,0:T(8,128)(2,1)}) custom-call(s32[16]{0:T(128)S(1)} %copy-done, ...), custom_call_target="tpu_custom_call", output_to_operand_aliasing={{1}: (3, {}), {2}: (4, {})} | custom-call | tf_op jit(solution)/shard_map/attend/pallas_call | solution.py:458
  23.3 38.7 %output.1 = bf16[3,4,2,8,6144]{4,3,2,1,0:T(8,128)(2,1)S(1)} custom-call(s32[16]{0:T(128)S(1)} %copy-done, bf16[4,3,16,1536]{3,2,1,0:T(8,128)(2,1)S(1)} %get-tuple-element.12.q_ref, bf16[16,2048,128]{2,1,0:T(8,128)(2,1)S(1)} %get-tuple-element.16.k_buf, bf16[16,2048,128]{2,1,0:T(8,128)(2,1)S(1)} %get-tuple-element.17.v_buf, ...), custom_call_target="tpu_custom_call" | custom-call | tf_op jit(solution)/shard_map/output/pallas_call | solution.py:480
  62.0 1.4 %emit.1 = bf16[3,64,6144]{2,1,0:T(8,128)(2,1)} custom-call(bf16[3,64,6144]{2,1,0:T(8,128)(2,1)S(1)} %bitcast.3), custom_call_target="tpu_custom_call" | custom-call | tf_op jit(solution)/shard_map/emit/pallas_call | solution.py:496
Async XLA Ops:
  0.6 15.8 %copy-start = (s32[16]{0:T(128)S(1)}, s32[16]{0:T(128)}, u32[]{:S(2)}) copy-start(s32[16]{0:T(128)} %lens_ref.3) | copy-start | bytes 196

commit v2 on v1

--- a/solution.py
+++ b/solution.py
@@ -33,7 +33,8 @@
 def project_kernel(dims, x_hbm, gain_hbm, bias_hbm, wq_hbm, bq_hbm, wkv_hbm, bkv_hbm, k_hbm, v_hbm,
                    q_ref, kv_ref, k_buf, v_buf,
                    x_buf, normed, wq_buf, wkv_buf, q_send, gain_ref, bias_ref, bq_ref, bkv_ref,
-                   x_sem, wq_sem, wkv_sem, cache_sem, vec_sem, send_sem, recv_sem):
+                   x_sem, wq_sem, wkv_sem, cache_sem, vec_sem, send_sem, recv_sem,
+                   kv_send, kv_send_sem, kv_recv_sem):
     n_steps, group_rows, tp_size, n_chunks, block = dims
     local_rows = group_rows // tp_size
     n_rows, d_model = x_buf.shape
@@ -42,6 +43,9 @@
     width = wq_buf.shape[2]
     first_chunks = n_chunks // 2
     me = lax.axis_index("tp")
+    chip, core = me // 2, lax.rem(me, 2)
+    partner = chip * 2 + (1 - core)
+    head_dim = wkv_buf.shape[1]
 
     def x_copy(idx):
         rows = pl.ds(pl.multiple_of(idx * block, block), block)
@@ -57,7 +61,8 @@
     vec_copies = [pltpu.make_async_copy(src, dst, vec_sem.at[idx]) for idx, (src, dst) in enumerate(vectors)]
     for copy in vec_copies:
         copy.start()
-    late_copies = [pltpu.make_async_copy(wkv_hbm, wkv_buf, wkv_sem)]
+    kv_cols = pl.ds(pl.multiple_of(core * head_dim, LANES), head_dim)
+    late_copies = [pltpu.make_async_copy(wkv_hbm.at[:, kv_cols], wkv_buf, wkv_sem)]
     for idx, (src, dst) in enumerate(((k_hbm, k_buf), (v_hbm, v_buf))):
         late_copies.append(pltpu.make_async_copy(src, dst, cache_sem.at[idx]))
     barrier = greet(me, tp_size)
@@ -93,6 +98,7 @@
         return carry
 
     lax.fori_loop(0, n_blocks, norm_block, 0)
+    late_copies[0].start()
     for chunk in range(first_chunks, n_chunks):
         wq_copy(chunk).start()
     pl.semaphore_wait(barrier, tp_size - 1)
@@ -108,9 +114,9 @@
     def q_chunk(chunk, carry):
         wq_copy(chunk).wait()
 
-        @pl.when(chunk == first_chunks)
+        @pl.when(chunk == 1)
         def _():
-            for copy in late_copies:
+            for copy in late_copies[1:]:
                 copy.start()
 
         cols = pl.ds(pl.multiple_of(chunk * width, LANES), width)
@@ -125,13 +131,18 @@
     lax.fori_loop(0, n_chunks, q_chunk, 0)
 
     late_copies[0].wait()
-    own_rows = [normed[pl.ds(pl.multiple_of(step * group_rows + me * local_rows, local_rows), local_rows), :] for step in range(n_steps)]
-    own_normed = jnp.concatenate(own_rows, axis=0)
-    kv_rows = jnp.dot(own_normed, wkv_buf[...], preferred_element_type=F32) + bkv_ref[...].astype(F32)[None]
-    kv_rows = kv_rows.astype(BF16).astype(F32)
-    head_dim = kv_ref.shape[2]
-    kv_ref[0] = kv_rows[:, :head_dim]
-    kv_ref[1] = kv_rows[:, head_dim:]
+    pair_rows = 2 * local_rows
+    parts = [normed[pl.ds(pl.multiple_of(step * group_rows + chip * pair_rows, pair_rows), pair_rows), :] for step in range(n_steps)]
+    kv_rows = jnp.dot(jnp.concatenate(parts, axis=0), wkv_buf[...], preferred_element_type=F32)
+    kv_bias = jnp.where(core == 0, bkv_ref[:head_dim].astype(F32), bkv_ref[head_dim:].astype(F32))
+    kv_rows = (kv_rows + kv_bias[None]).astype(BF16).astype(F32)
+    kv_send[...] = kv_rows.reshape(n_steps, 2, local_rows, head_dim)
+
+    def kv_copy(half, target):
+        return send(kv_send.at[:, 1 - half], kv_ref.at[half], kv_send_sem, kv_recv_sem, target)
+
+    kv_copy(core, partner).start()
+    kv_ref[core] = kv_send[:, core]
 
     def drain(chunk, carry):
         for shift in range(1, tp_size):
@@ -140,35 +151,49 @@
         return carry
 
     lax.fori_loop(0, n_chunks, drain, 0)
+    kv_copy(core, partner).wait_send()
+    kv_copy(1 - core, partner).wait_recv()
     for copy in late_copies[1:]:
         copy.wait()
 
 
-def attend_set(first_seq, lens_ref, q_ref, k_buf, v_buf, a_ref, q_rows, o_rows, scores_a, scores_b, max_a, max_b):
-    n_steps, n_seqs, _ = a_ref.shape
-    _, cache_len, head_dim = k_buf.shape
-    n_src, _, _, src_width = q_ref.shape
+def spread_heads(q_ref, q_rows):
+    n_src, n_steps, n_seqs, src_width = q_ref.shape
+    head_dim = q_rows.shape[1]
     src_heads = src_width // head_dim
-    n_heads = n_src * src_heads
-    n_rows = n_steps * n_heads
+    for src in range(n_src):
+        for step in range(n_steps):
+            for head in range(src_heads):
+                row = (step * n_src * src_heads + src * src_heads + head) * n_seqs
+                q_rows[row:row + n_seqs, :] = q_ref[src, step, :, head * head_dim:(head + 1) * head_dim].astype(F32)
+
+
+def gather_heads(first_seq, o_rows, a_ref):
+    n_steps, set_rows, width = a_ref.shape
+    head_dim = o_rows.shape[1]
+    n_heads = width // head_dim
+    n_seqs = o_rows.shape[0] // (n_steps * n_heads)
+    for step in range(n_steps):
+        for head in range(n_heads):
+            row = (step * n_heads + head) * n_seqs + first_seq
+            a_ref[step, :, head * head_dim:(head + 1) * head_dim] = o_rows[row:row + set_rows, :].astype(BF16)
+
+
+def attend_range(first_seq, last_seq, n_steps, lens_ref, q_rows, k_buf, v_buf, o_rows, scores_a, scores_b, max_a, max_b):
+    n_seqs, cache_len, head_dim = k_buf.shape
+    n_rows = q_rows.shape[0] // n_seqs
+    n_heads = n_rows // n_steps
     scale = head_dim ** -0.5 * LOG2E
     key_block = 256
     n_blocks = cache_len // key_block
 
-    for src in range(n_src):
-        for step in range(n_steps):
-            for head in range(src_heads):
-                row = (step * n_heads + src * src_heads + head) * n_seqs
-                heads = q_ref[src, step, first_seq:first_seq + n_seqs, head * head_dim:(head + 1) * head_dim]
-                q_rows[row:row + n_seqs, :] = heads.astype(F32)
-
     def score_stage(seq, scores, max_ref):
-        length = lens_ref[first_seq + seq]
+        length = lens_ref[seq]
         queries = q_rows[pl.ds(seq, n_rows, stride=n_seqs), :].astype(BF16)
         lane = lax.broadcasted_iota(jnp.int32, (n_heads, key_block), 1)
         best = jnp.full((n_rows, LANES), -jnp.inf, F32)
         for block in range(n_blocks):
-            keys = k_buf[first_seq + seq, block * key_block:(block + 1) * key_block, :]
+            keys = k_buf[seq, block * key_block:(block + 1) * key_block, :]
             part = lax.dot_general(queries, keys, (((1,), (1,)), ((), ())), preferred_element_type=F32)
             masked = []
             for step in range(n_steps):
@@ -191,35 +216,32 @@
                 weight = jnp.exp2(scores[:, start:start + LANES] * scale - top)
                 denom = denom + weight
                 parts.append(weight.astype(BF16))
-            values = v_buf[first_seq + seq, block * key_block:(block + 1) * key_block, :]
+            values = v_buf[seq, block * key_block:(block + 1) * key_block, :]
             numer = numer + jnp.dot(jnp.concatenate(parts, axis=1), values, preferred_element_type=F32)
         o_rows[pl.ds(seq, n_rows, stride=n_seqs), :] = numer / jnp.sum(denom, axis=1, keepdims=True)
 
-    score_stage(0, scores_a, max_a)
+    score_stage(first_seq, scores_a, max_a)
 
     def pair(idx, carry):
-        seq = idx * 2
+        seq = first_seq + idx * 2
         score_stage(seq + 1, scores_b, max_b)
         value_stage(seq, scores_a, max_a)
         score_stage(seq + 2, scores_a, max_a)
         value_stage(seq + 1, scores_b, max_b)
         return carry
 
-    lax.fori_loop(0, n_seqs // 2 - 1, pair, 0)
-    score_stage(n_seqs - 1, scores_b, max_b)
-    value_stage(n_seqs - 2, scores_a, max_a)
-    value_stage(n_seqs - 1, scores_b, max_b)
-
-    for step in range(n_steps):
-        for head in range(n_heads):
-            row = (step * n_heads + head) * n_seqs
-            a_ref[step, :, head * head_dim:(head + 1) * head_dim] = o_rows[row:row + n_seqs, :].astype(BF16)
-
-
-def attend_kernel(lens_ref, q_ref, kv_ref, k_in, v_in,
-                  a_ref, k_buf, v_buf, k_out, v_out,
-                  q_rows, o_rows, scores_a, scores_b, max_a, max_b, out_sem):
+    lax.fori_loop(0, (last_seq - first_seq) // 2 - 1, pair, 0)
+    score_stage(last_seq - 1, scores_b, max_b)
+    value_stage(last_seq - 2, scores_a, max_a)
+    value_stage(last_seq - 1, scores_b, max_b)
+
+
+def attend_kernel(n_first, lens_hbm, q_ref, kv_ref, k_in, v_in,
+                  a_ref, q_rows, o_rows, k_buf, v_buf, k_out, v_out,
+                  scores_a, scores_b, max_a, max_b, out_sem, lens_ref, lens_sem):
     del k_in, v_in
+    lens_copy = pltpu.make_async_copy(lens_hbm, lens_ref, lens_sem)
+    lens_copy.start()
     n_seqs, cache_len, head_dim = k_buf.shape
     n_steps = a_ref.shape[0]
 
@@ -235,7 +257,7 @@
         for buf_idx, buf in enumerate((k_buf, v_buf)):
             rows = buf[seq, window, :].astype(F32)
             for step in range(n_steps):
-                fresh = kv_ref[buf_idx, pl.ds(step * n_seqs + seq, 1), :]
+                fresh = kv_ref[buf_idx, step, pl.ds(seq, 1), :]
                 rows = jnp.where(positions == length + step, fresh, rows)
             buf[seq, window, :] = rows.astype(BF16)
         return carry
@@ -250,9 +272,20 @@
         store(1, seq).wait()
         return carry
 
-    lax.fori_loop(0, n_seqs, update, 0)
-    lax.fori_loop(0, n_seqs, write, 0)
-    attend_set(0, lens_ref, q_ref, k_buf, v_buf, a_ref, q_rows, o_rows, scores_a, scores_b, max_a, max_b)
+    def refresh(seq, carry):
+        update(seq, carry)
+
+        @pl.when(seq > 0)
+        def _():
+            write(seq - 1, carry)
+        return carry
+
+    spread_heads(q_ref, q_rows)
+    lens_copy.wait()
+    lax.fori_loop(0, n_seqs, refresh, 0)
+    write(n_seqs - 1, 0)
+    attend_range(0, n_first, n_steps, lens_ref, q_rows, k_buf, v_buf, o_rows, scores_a, scores_b, max_a, max_b)
+    gather_heads(0, o_rows, a_ref)
     lax.fori_loop(0, n_seqs, finish, 0)
 
 
@@ -262,13 +295,13 @@
     copy.wait()
 
 
-def output_kernel(dims, lens_ref, q_ref, k_buf, v_buf, a_first, x_hbm, wo_hbm, bo_hbm,
+def output_kernel(dims, lens_hbm, q_rows, o_first, k_buf, v_buf, a_first, x_hbm, wo_hbm, bo_hbm,
                   y_ref,
                   bo_ref, a_second, a_recv, wo_buf, pair_send, pair_recv, chip_sum, chip_recv,
-                  q_rows, o_rows, scores_a, scores_b, max_a, max_b,
+                  o_rows, scores_a, scores_b, max_a, max_b,
                   x_sem, bo_sem, wo_sem, a_send_sem, a_recv_sem, pair_send_sem, pair_recv_sem,
-                  chip_send_sem, chip_recv_sem, y_send_sem, y_recv_sem):
-    tp_size, n_chunks, lag = dims
+                  chip_send_sem, chip_recv_sem, y_send_sem, y_recv_sem, lens_ref, lens_sem):
+    tp_size, n_chunks, lag, n_first = dims
     n_steps, set_rows, _ = a_first.shape
     depth = wo_buf.shape[1]
     width = wo_buf.shape[2]
@@ -279,6 +312,8 @@
     partner = chip * 2 + (1 - core)
     across = (1 - chip) * 2 + core
     barrier = greet(me, tp_size)
+    lens_copy = pltpu.make_async_copy(lens_hbm, lens_ref, lens_sem)
+    lens_copy.start()
 
     def wo_copy(chunk):
         cols = pl.ds(pl.multiple_of(chunk * width, LANES), width)
@@ -353,7 +388,14 @@
 
     pl.semaphore_wait(barrier, tp_size - 1)
     exchange(0)
-    attend_set(set_rows, lens_ref, q_ref, k_buf, v_buf, a_second, q_rows, o_rows, scores_a, scores_b, max_a, max_b)
+    n_seqs = k_buf.shape[0]
+    n_rows = q_rows.shape[0] // n_seqs
+    for seq in range(set_rows, n_first):
+        rows = pl.ds(seq, n_rows, stride=n_seqs)
+        o_rows[rows, :] = o_first[rows, :]
+    lens_copy.wait()
+    attend_range(n_first, n_seqs, n_steps, lens_ref, q_rows, k_buf, v_buf, o_rows, scores_a, scores_b, max_a, max_b)
+    gather_heads(set_rows, o_rows, a_second)
     exchange(1)
     received(0)
     project(0)
@@ -425,7 +467,7 @@
             functools.partial(project_kernel, (n_steps, group_rows, tp_size, q_chunks, block)),
             out_shape=(
                 VMEM((tp_size, n_steps, local_rows, q_cols), BF16),
-                VMEM((2, n_steps * local_rows, head_dim), F32),
+                VMEM((2, n_steps, local_rows, head_dim), F32),
                 VMEM(k_cache.shape, BF16),
                 VMEM(v_cache.shape, BF16),
             ),
@@ -435,10 +477,11 @@
                 VMEM((n_x, d_model), BF16),
                 VMEM((n_x, d_model), BF16),
                 VMEM((q_chunks, d_model, q_cols // q_chunks), BF16),
-                VMEM((d_model, 2 * head_dim), BF16),
+                VMEM((d_model, head_dim), BF16),
                 VMEM((n_steps, group_rows, q_cols), BF16),
                 VMEM(ln_gain.shape, BF16), VMEM(ln_bias.shape, BF16), VMEM(b_q.shape, BF16), VMEM(b_kv.shape, BF16),
                 dma((n_x // block,)), dma((q_chunks,)), dma, dma((2,)), dma((4,)), remote, remote,
+                VMEM((n_steps, 2, local_rows, head_dim), F32), dma, dma,
             ],
             compiler_params=pltpu.CompilerParams(collective_id=0, has_side_effects=True, vmem_limit_bytes=31 * mib),
             name="project",
@@ -446,31 +489,33 @@
 
         n_rows = n_steps * n_heads
         set_rows = local_rows // 2
+        n_first = 10
+        spread = VMEM((n_rows * local_rows, head_dim), F32)
         attend_scratch = [
-            VMEM((n_rows * set_rows, head_dim), F32),
-            VMEM((n_rows * set_rows, head_dim), F32),
             VMEM((n_rows, cache_len), F32),
             VMEM((n_rows, cache_len), F32),
             VMEM((n_rows, LANES), F32),
             VMEM((n_rows, LANES), F32),
         ]
         a_set = (n_steps, set_rows, n_heads * head_dim)
-        a_first, k_held, v_held, k_new, v_new = pl.pallas_call(
-            attend_kernel,
+        a_first, q_rows, o_rows, k_held, v_held, k_new, v_new = pl.pallas_call(
+            functools.partial(attend_kernel, n_first),
             out_shape=(
                 VMEM(a_set, BF16),
+                spread,
+                spread,
                 VMEM(k_cache.shape, BF16),
                 VMEM(v_cache.shape, BF16),
                 jax.ShapeDtypeStruct(k_cache.shape, BF16),
                 jax.ShapeDtypeStruct(v_cache.shape, BF16),
             ),
-            in_specs=[spec(pltpu.SMEM)] + [spec(VMEM)] * 4,
-            out_specs=(spec(VMEM),) * 3 + (spec(pl.ANY),) * 2,
-            input_output_aliases={3: 1, 4: 2},
-            scratch_shapes=attend_scratch + [dma((2, local_rows))],
+            in_specs=[spec(pl.ANY)] + [spec(VMEM)] * 4,
+            out_specs=(spec(VMEM),) * 5 + (spec(pl.ANY),) * 2,
+            input_output_aliases={3: 3, 4: 4},
+            scratch_shapes=attend_scratch + [dma((2, local_rows)), pltpu.SMEM((local_rows,), jnp.int32), dma],
             compiler_params=pltpu.CompilerParams(vmem_limit_bytes=12 * mib),
             name="attend",
-        )(seq_lens, q_blocks, kv_rows, k_held, v_held)
+        )(in_hbm(seq_lens), q_blocks, kv_rows, k_held, v_held)
 
         o_chunks = 6
         n_units = 2 * o_chunks
@@ -478,21 +523,22 @@
         units = (n_units, n_steps * tp_size * set_rows, width)
         split = (n_steps, tp_size, 2, set_rows, d_model)
         y_held = pl.pallas_call(
-            functools.partial(output_kernel, (tp_size, o_chunks, 3)),
+            functools.partial(output_kernel, (tp_size, o_chunks, 3, n_first)),
             out_shape=VMEM(split, BF16),
-            in_specs=[spec(pltpu.SMEM)] + [spec(VMEM)] * 4 + [spec(pl.ANY)] * 3,
+            in_specs=[spec(pl.ANY)] + [spec(VMEM)] * 5 + [spec(pl.ANY)] * 3,
             out_specs=spec(VMEM),
             scratch_shapes=[
                 VMEM(b_out.shape, BF16), VMEM(a_set, BF16),
                 VMEM((2, n_steps, tp_size, set_rows, q_cols), BF16),
                 VMEM((n_units, q_cols, width), BF16),
                 VMEM(units, BF16), VMEM(units, BF16), VMEM(units, BF16), VMEM(units, BF16),
+                spread,
             ] + attend_scratch + [
                 dma, dma, dma((n_units,)), dma((2, tp_size - 1)), dma((2, tp_size - 1)),
-            ] + [dma((n_units,))] * 6,
+            ] + [dma((n_units,))] * 6 + [pltpu.SMEM((local_rows,), jnp.int32), dma],
             compiler_params=pltpu.CompilerParams(collective_id=1, has_side_effects=True, vmem_limit_bytes=31 * mib),
             name="output",
-        )(seq_lens, q_blocks, k_held, v_held, a_first, in_hbm(x_steps.reshape(split)), in_hbm(w_out), in_hbm(b_out))
+        )(in_hbm(seq_lens), q_rows, o_rows, k_held, v_held, a_first, in_hbm(x_steps.reshape(split)), in_hbm(w_out), in_hbm(b_out))
         y_steps = pl.pallas_call(
             emit_kernel,
             out_shape=jax.ShapeDtypeStruct(x_steps.shape, BF16),

time: 63.6 us -> 62.8 us (0.987)
  Pallas kernels: 62.8 us -> 62 us
    pallas_call x2, Pallas kernels: 45.6 us -> 44.8 us  [the longest x1 37.6 us: local_block(): pl.pallas_call(functools.partial(output_kernel, (tp_size, o_chunks, 3, n_...]
where the time goes in v2:
time: 62.8 us; the launch traced here: 62.6 us
  Pallas kernels  62 us (99%)
  between operations  0.66 us (1%)
    pallas_call x1, Pallas kernels, local_block(): pl.pallas_call(functools.partial(output_kernel, (tp_size, o_chunks, 3, n_...  37.6 us
    pallas_call x1, Pallas kernels, local_block(): pl.pallas_call(functools.partial(project_kernel, (n_steps, group_rows, tp...  15.8 us
    pallas_call x1, Pallas kernels, local_block(): pl.pallas_call(functools.partial(attend_kernel, n_first), out_shape=(VMEM...  7.2 us
    pallas_call x1, Pallas kernels, local_block(): pl.pallas_call(emit_kernel, out_shape=jax.ShapeDtypeStruct(x_steps.shape,...  1.42 us

profile of v2, /device:TPU:0, one launch (start us, length us, event | category | flops | bytes accessed | tf_op | source)
XLA Modules:
  0.0 62.6 jit_solution(11088303819234523669)
XLA Ops:
  0.6 15.8 %project.1 = (bf16[4,3,16,1536]{3,2,1,0:T(8,128)(2,1)S(1)}, f32[2,3,16,128]{3,2,1,0:T(8,128)S(1)}, bf16[16,2048,128]{2,1,0:T(8,128)(2,1)S(1)}, bf16[16,2048,128]{2,1,0:T(8,128)(2,1)S(1)}) custom-call(bf16[192,6144]{1,0:T(8,128)(2,1)} %bitcast.4, bf16[6144]{0:T(1024)(128)(2,1)} %gain_hbm.1, bf16[6144]{0:T(1024)(128)(2,1)} %bias_hbm.1, ...), custom_call_target="tpu_custom_call" | custom-call | tf_op jit(solution)/shard_map/project/pallas_call | solution.py:466
  16.4 7.2 %attend.1 = (bf16[3,8,6144]{2,1,0:T(8,128)(2,1)S(1)}, f32[2304,128]{1,0:T(8,128)S(1)}, f32[2304,128]{1,0:T(8,128)S(1)}, bf16[16,2048,128]{2,1,0:T(8,128)(2,1)S(1...) custom-call(s32[16]{0:T(128)} %lens_hbm.3, ...), custom_call_target="tpu_custom_call", output_to_operand_aliasing={{3}: (3, {}), {4}: (4, {})} | custom-call | tf_op jit(solution)/shard_map/attend/pallas_call | solution.py:501
  23.6 37.6 %output.1 = bf16[3,4,2,8,6144]{4,3,2,1,0:T(8,128)(2,1)S(1)} custom-call(s32[16]{0:T(128)} %lens_hbm.3, f32[2304,128]{1,0:T(8,128)S(1)} %get-tuple-element.18.q_rows, f32[2304,128]{1,0:T(8,128)S(1)} %get-tuple-element.19.o_first, bf16[16,2048,128]{2,1,0:T(8,128)(2,1)S(1)} %get-tuple-element.20.k_buf, bf16[16,2048,128]{2,1,0:T(8,128)(2,1)S(1)} %get-tuple-element.21.v_buf, ...), custom_call_target="tpu_custom_call" | custom-call | tf_op jit(solution)/shard_map/output/pallas_call | solution.py:525
  61.2 1.4 %emit.1 = bf16[3,64,6144]{2,1,0:T(8,128)(2,1)} custom-call(bf16[3,64,6144]{2,1,0:T(8,128)(2,1)S(1)} %bitcast.3), custom_call_target="tpu_custom_call" | custom-call | tf_op jit(solution)/shard_map/emit/pallas_call | solution.py:542

commit v3 on v2

--- a/solution.py
+++ b/solution.py
@@ -30,12 +30,24 @@
     return barrier
 
 
+def spread_heads(chunk, q_ref, q_rows):
+    n_chunks, n_src, n_steps, n_seqs, width = q_ref.shape
+    head_dim = q_rows.shape[1]
+    chunk_heads = width // head_dim
+    for src in range(n_src):
+        for step in range(n_steps):
+            for idx in range(chunk_heads):
+                head = (src * n_chunks + chunk) * chunk_heads + idx
+                row = (step * n_src * n_chunks * chunk_heads + head) * n_seqs
+                q_rows[row:row + n_seqs, :] = q_ref[chunk, src, step, :, idx * head_dim:(idx + 1) * head_dim].astype(F32)
+
+
 def project_kernel(dims, x_hbm, gain_hbm, bias_hbm, wq_hbm, bq_hbm, wkv_hbm, bkv_hbm, k_hbm, v_hbm,
-                   q_ref, kv_ref, k_buf, v_buf,
-                   x_buf, normed, wq_buf, wkv_buf, q_send, gain_ref, bias_ref, bq_ref, bkv_ref,
+                   q_rows, kv_ref, k_buf, v_buf,
+                   x_buf, normed, wq_buf, wkv_buf, q_send, q_ref, gain_ref, bias_ref, bq_ref, bkv_ref,
                    x_sem, wq_sem, wkv_sem, cache_sem, vec_sem, send_sem, recv_sem,
                    kv_send, kv_send_sem, kv_recv_sem):
-    n_steps, group_rows, tp_size, n_chunks, block = dims
+    n_steps, group_rows, tp_size, n_chunks, block, n_early = dims
     local_rows = group_rows // tp_size
     n_rows, d_model = x_buf.shape
     n_blocks = n_rows // block
@@ -64,7 +76,8 @@
     kv_cols = pl.ds(pl.multiple_of(core * head_dim, LANES), head_dim)
     late_copies = [pltpu.make_async_copy(wkv_hbm.at[:, kv_cols], wkv_buf, wkv_sem)]
     for idx, (src, dst) in enumerate(((k_hbm, k_buf), (v_hbm, v_buf))):
-        late_copies.append(pltpu.make_async_copy(src, dst, cache_sem.at[idx]))
+        early = pl.ds(0, n_early)
+        late_copies.append(pltpu.make_async_copy(src.at[early], dst.at[early], cache_sem.at[idx]))
     barrier = greet(me, tp_size)
     for copy in vec_copies:
         copy.wait()
@@ -105,11 +118,7 @@
 
     def q_copy(chunk, shift, origin):
         target = lax.rem(origin + shift, tp_size)
-        cols = pl.ds(pl.multiple_of(chunk * width, LANES), width)
-        return send(
-            q_send.at[:, pl.ds(pl.multiple_of(target * local_rows, local_rows), local_rows), cols],
-            q_ref.at[origin, :, :, cols],
-            send_sem.at[chunk, shift - 1], recv_sem.at[chunk, shift - 1], target)
+        return send(q_send.at[chunk, target], q_ref.at[chunk, origin], send_sem.at[chunk, shift - 1], recv_sem.at[chunk, shift - 1], target)
 
     def q_chunk(chunk, carry):
         wq_copy(chunk).wait()
@@ -121,11 +130,13 @@
 
         cols = pl.ds(pl.multiple_of(chunk * width, LANES), width)
         part = jnp.dot(normed[...], wq_buf[chunk], preferred_element_type=F32) + bq_ref[cols].astype(F32)[None]
-        q_send[:, :, cols] = part.astype(BF16).reshape(n_steps, group_rows, width)
+        for target in range(tp_size):
+            for step in range(n_steps):
+                row = step * group_rows + target * local_rows
+                q_send[chunk, target, step] = part[row:row + local_rows, :].astype(BF16)
         for shift in (2, 3, 1):
             q_copy(chunk, shift, me).start()
-        own = pl.ds(pl.multiple_of(me * local_rows, local_rows), local_rows)
-        q_ref[me, :, :, cols] = q_send[:, own, cols]
+        q_ref[chunk, me] = q_send[chunk, me]
         return carry
 
     lax.fori_loop(0, n_chunks, q_chunk, 0)
@@ -144,28 +155,17 @@
     kv_copy(core, partner).start()
     kv_ref[core] = kv_send[:, core]
 
-    def drain(chunk, carry):
+    for chunk in range(n_chunks):
+        for shift in range(1, tp_size):
+            q_copy(chunk, shift, lax.rem(me - shift + tp_size, tp_size)).wait_recv()
+        spread_heads(chunk, q_ref, q_rows)
+    for chunk in range(n_chunks):
         for shift in range(1, tp_size):
             q_copy(chunk, shift, me).wait_send()
-            q_copy(chunk, shift, lax.rem(me - shift + tp_size, tp_size)).wait_recv()
-        return carry
-
-    lax.fori_loop(0, n_chunks, drain, 0)
     kv_copy(core, partner).wait_send()
     kv_copy(1 - core, partner).wait_recv()
     for copy in late_copies[1:]:
         copy.wait()
-
-
-def spread_heads(q_ref, q_rows):
-    n_src, n_steps, n_seqs, src_width = q_ref.shape
-    head_dim = q_rows.shape[1]
-    src_heads = src_width // head_dim
-    for src in range(n_src):
-        for step in range(n_steps):
-            for head in range(src_heads):
-                row = (step * n_src * src_heads + src * src_heads + head) * n_seqs
-                q_rows[row:row + n_seqs, :] = q_ref[src, step, :, head * head_dim:(head + 1) * head_dim].astype(F32)
 
 
 def gather_heads(first_seq, o_rows, a_ref):
@@ -179,7 +179,7 @@
             a_ref[step, :, head * head_dim:(head + 1) * head_dim] = o_rows[row:row + set_rows, :].astype(BF16)
 
 
-def attend_range(first_seq, last_seq, n_steps, lens_ref, q_rows, k_buf, v_buf, o_rows, scores_a, scores_b, max_a, max_b):
+def attend_range(first_seq, last_seq, n_steps, lens_ref, q_rows, k_buf, v_buf, o_rows, scores_a, scores_b, max_a, max_b, aside=None, skip=False):
     n_seqs, cache_len, head_dim = k_buf.shape
     n_rows = q_rows.shape[0] // n_seqs
     n_heads = n_rows // n_steps
@@ -187,7 +187,7 @@
     key_block = 256
     n_blocks = cache_len // key_block
 
-    def score_stage(seq, scores, max_ref):
+    def score_stage(seq, scores, max_ref, n_blocks=n_blocks):
         length = lens_ref[seq]
         queries = q_rows[pl.ds(seq, n_rows, stride=n_seqs), :].astype(BF16)
         lane = lax.broadcasted_iota(jnp.int32, (n_heads, key_block), 1)
@@ -205,7 +205,7 @@
                 best = jnp.maximum(best, part[:, idx * LANES:(idx + 1) * LANES])
         max_ref[...] = jnp.broadcast_to(jnp.max(best, axis=1, keepdims=True) * scale, (n_rows, LANES))
 
-    def value_stage(seq, scores, max_ref):
+    def value_stage(seq, scores, max_ref, n_blocks=n_blocks):
         top = max_ref[...]
         denom = jnp.zeros((n_rows, LANES), F32)
         numer = jnp.zeros((n_rows, head_dim), F32)
@@ -220,30 +220,58 @@
             numer = numer + jnp.dot(jnp.concatenate(parts, axis=1), values, preferred_element_type=F32)
         o_rows[pl.ds(seq, n_rows, stride=n_seqs), :] = numer / jnp.sum(denom, axis=1, keepdims=True)
 
+    def overlap(score_seq, score_buf, score_max, value_seq, value_buf, value_max):
+        if not skip:
+            score_stage(score_seq, score_buf, score_max)
+            value_stage(value_seq, value_buf, value_max)
+            return
+        score_short = lens_ref[score_seq] + n_steps <= cache_len // 2
+        value_short = lens_ref[value_seq] + n_steps <= cache_len // 2
+        for score_blocks, score_case in ((n_blocks // 2, score_short), (n_blocks, jnp.logical_not(score_short))):
+            for value_blocks, value_case in ((n_blocks // 2, value_short), (n_blocks, jnp.logical_not(value_short))):
+                @pl.when(score_case & value_case)
+                def _():
+                    score_stage(score_seq, score_buf, score_max, score_blocks)
+                    value_stage(value_seq, value_buf, value_max, value_blocks)
+
     score_stage(first_seq, scores_a, max_a)
 
     def pair(idx, carry):
+        if aside is not None:
+            pl.when(idx == 2)(aside)
         seq = first_seq + idx * 2
-        score_stage(seq + 1, scores_b, max_b)
-        value_stage(seq, scores_a, max_a)
-        score_stage(seq + 2, scores_a, max_a)
-        value_stage(seq + 1, scores_b, max_b)
+        overlap(seq + 1, scores_b, max_b, seq, scores_a, max_a)
+        overlap(seq + 2, scores_a, max_a, seq + 1, scores_b, max_b)
         return carry
 
     lax.fori_loop(0, (last_seq - first_seq) // 2 - 1, pair, 0)
-    score_stage(last_seq - 1, scores_b, max_b)
-    value_stage(last_seq - 2, scores_a, max_a)
-    value_stage(last_seq - 1, scores_b, max_b)
-
-
-def attend_kernel(n_first, lens_hbm, q_ref, kv_ref, k_in, v_in,
-                  a_ref, q_rows, o_rows, k_buf, v_buf, k_out, v_out,
-                  scores_a, scores_b, max_a, max_b, out_sem, lens_ref, lens_sem):
+    if not skip:
+        score_stage(last_seq - 1, scores_b, max_b)
+        value_stage(last_seq - 2, scores_a, max_a)
+        value_stage(last_seq - 1, scores_b, max_b)
+        return
+    overlap(last_seq - 1, scores_b, max_b, last_seq - 2, scores_a, max_a)
+    last_short = lens_ref[last_seq - 1] + n_steps <= cache_len // 2
+    for blocks, case in ((n_blocks // 2, last_short), (n_blocks, jnp.logical_not(last_short))):
+        @pl.when(case)
+        def _():
+            value_stage(last_seq - 1, scores_b, max_b, blocks)
+
+
+def attend_kernel(dims, lens_hbm, q_rows, kv_ref, k_in, v_in, k_hbm, v_hbm,
+                  a_ref, o_rows, k_buf, v_buf, k_out, v_out,
+                  scores_a, scores_b, max_a, max_b, out_sem, lens_ref, lens_sem, late_sem):
     del k_in, v_in
+    n_first, n_early = dims
     lens_copy = pltpu.make_async_copy(lens_hbm, lens_ref, lens_sem)
     lens_copy.start()
     n_seqs, cache_len, head_dim = k_buf.shape
     n_steps = a_ref.shape[0]
+
+    late = pl.ds(n_early, n_seqs - n_early)
+    late_copies = [pltpu.make_async_copy(src.at[late], dst.at[late], late_sem.at[idx]) for idx, (src, dst) in enumerate(((k_hbm, k_buf), (v_hbm, v_buf)))]
+    for copy in late_copies:
+        copy.start()
 
     def store(buf_idx, seq):
         src, dst = ((k_buf, k_out), (v_buf, v_out))[buf_idx]
@@ -275,16 +303,21 @@
     def refresh(seq, carry):
         update(seq, carry)
 
-        @pl.when(seq > 0)
+        @pl.when((seq > 0) & (seq != n_early))
         def _():
             write(seq - 1, carry)
         return carry
 
-    spread_heads(q_ref, q_rows)
+    def refresh_late():
+        for copy in late_copies:
+            copy.wait()
+        lax.fori_loop(n_early, n_seqs, refresh, 0)
+        write(n_seqs - 1, 0)
+
     lens_copy.wait()
-    lax.fori_loop(0, n_seqs, refresh, 0)
-    write(n_seqs - 1, 0)
-    attend_range(0, n_first, n_steps, lens_ref, q_rows, k_buf, v_buf, o_rows, scores_a, scores_b, max_a, max_b)
+    lax.fori_loop(0, n_early, refresh, 0)
+    write(n_early - 1, 0)
+    attend_range(0, n_first, n_steps, lens_ref, q_rows, k_buf, v_buf, o_rows, scores_a, scores_b, max_a, max_b, refresh_late, True)
     gather_heads(0, o_rows, a_ref)
     lax.fori_loop(0, n_seqs, finish, 0)
 
@@ -462,11 +495,14 @@
         dma = pltpu.SemaphoreType.DMA
 
         q_chunks, block = 6, 32
+        n_first, n_early = 10, 14
         remote = dma((q_chunks, tp_size - 1))
-        q_blocks, kv_rows, k_held, v_held = pl.pallas_call(
-            functools.partial(project_kernel, (n_steps, group_rows, tp_size, q_chunks, block)),
+        n_rows = n_steps * n_heads
+        spread = VMEM((n_rows * local_rows, head_dim), F32)
+        q_rows, kv_rows, k_held, v_held = pl.pallas_call(
+            functools.partial(project_kernel, (n_steps, group_rows, tp_size, q_chunks, block, n_early)),
             out_shape=(
-                VMEM((tp_size, n_steps, local_rows, q_cols), BF16),
+                spread,
                 VMEM((2, n_steps, local_rows, head_dim), F32),
                 VMEM(k_cache.shape, BF16),
                 VMEM(v_cache.shape, BF16),
@@ -478,7 +514,8 @@
                 VMEM((n_x, d_model), BF16),
                 VMEM((q_chunks, d_model, q_cols // q_chunks), BF16),
                 VMEM((d_model, head_dim), BF16),
-                VMEM((n_steps, group_rows, q_cols), BF16),
+                VMEM((q_chunks, tp_size, n_steps, local_rows, q_cols // q_chunks), BF16),
+                VMEM((q_chunks, tp_size, n_steps, local_rows, q_cols // q_chunks), BF16),
                 VMEM(ln_gain.shape, BF16), VMEM(ln_bias.shape, BF16), VMEM(b_q.shape, BF16), VMEM(b_kv.shape, BF16),
                 dma((n_x // block,)), dma((q_chunks,)), dma, dma((2,)), dma((4,)), remote, remote,
                 VMEM((n_steps, 2, local_rows, head_dim), F32), dma, dma,
@@ -487,10 +524,7 @@
             name="project",
         )(*(in_hbm(arg) for arg in (x_steps.reshape(n_x, d_model), ln_gain, ln_bias, w_q, b_q, w_kv, b_kv, k_cache, v_cache)))
 
-        n_rows = n_steps * n_heads
         set_rows = local_rows // 2
-        n_first = 10
-        spread = VMEM((n_rows * local_rows, head_dim), F32)
         attend_scratch = [
             VMEM((n_rows, cache_len), F32),
             VMEM((n_rows, cache_len), F32),
@@ -498,24 +532,23 @@
             VMEM((n_rows, LANES), F32),
         ]
         a_set = (n_steps, set_rows, n_heads * head_dim)
-        a_first, q_rows, o_rows, k_held, v_held, k_new, v_new = pl.pallas_call(
-            functools.partial(attend_kernel, n_first),
+        a_first, o_rows, k_held, v_held, k_new, v_new = pl.pallas_call(
+            functools.partial(attend_kernel, (n_first, n_early)),
             out_shape=(
                 VMEM(a_set, BF16),
-                spread,
                 spread,
                 VMEM(k_cache.shape, BF16),
                 VMEM(v_cache.shape, BF16),
                 jax.ShapeDtypeStruct(k_cache.shape, BF16),
                 jax.ShapeDtypeStruct(v_cache.shape, BF16),
             ),
-            in_specs=[spec(pl.ANY)] + [spec(VMEM)] * 4,
-            out_specs=(spec(VMEM),) * 5 + (spec(pl.ANY),) * 2,
-            input_output_aliases={3: 3, 4: 4},
-            scratch_shapes=attend_scratch + [dma((2, local_rows)), pltpu.SMEM((local_rows,), jnp.int32), dma],
+            in_specs=[spec(pl.ANY)] + [spec(VMEM)] * 4 + [spec(pl.ANY)] * 2,
+            out_specs=(spec(VMEM),) * 4 + (spec(pl.ANY),) * 2,
+            input_output_aliases={3: 2, 4: 3},
+            scratch_shapes=attend_scratch + [dma((2, local_rows)), pltpu.SMEM((local_rows,), jnp.int32), dma, dma((2,))],
             compiler_params=pltpu.CompilerParams(vmem_limit_bytes=12 * mib),
             name="attend",
-        )(in_hbm(seq_lens), q_blocks, kv_rows, k_held, v_held)
+        )(in_hbm(seq_lens), q_rows, kv_rows, k_held, v_held, in_hbm(k_cache), in_hbm(v_cache))
 
         o_chunks = 6
         n_units = 2 * o_chunks

time: 62.8 us -> 62.3 us (level)
  Pallas kernels: 62 us -> 61.3 us
where the time goes in v3:
time: 62.3 us; the launch traced here: 62 us
  Pallas kernels  61.3 us (98%)
  between operations  0.66 us (1%)
    pallas_call x1, Pallas kernels, local_block(): pl.pallas_call(functools.partial(output_kernel, (tp_size, o_chunks, 3, n_...  37 us
    pallas_call x1, Pallas kernels, local_block(): pl.pallas_call(functools.partial(project_kernel, (n_steps, group_rows, tp...  15.8 us
    pallas_call x1, Pallas kernels, local_block(): pl.pallas_call(functools.partial(attend_kernel, (n_first, n_early)), out_...  7.12 us
    pallas_call x1, Pallas kernels, local_block(): pl.pallas_call(emit_kernel, out_shape=jax.ShapeDtypeStruct(x_steps.shape,...  1.42 us

profile of v3, /device:TPU:0, one launch (start us, length us, event | category | flops | bytes accessed | tf_op | source)
XLA Modules:
  0.0 62.0 jit_solution(11671730118685638759)
XLA Ops:
  0.6 15.8 %project.1 = (f32[2304,128]{1,0:T(8,128)S(1)}, f32[2,3,16,128]{3,2,1,0:T(8,128)S(1)}, bf16[16,2048,128]{2,1,0:T(8,128)(2,1)S(1)}, bf16[16,2048,128]{2,1,0:T(8,128)(2,1)S(1)}) custom-call(bf16[192,6144]{1,0:T(8,128)(2,1)} %bitcast.4, bf16[6144]{0:T(1024)(128)(2,1)} %gain_hbm.1, bf16[6144]{0:T(1024)(128)(2,1)} %bias_hbm.1, bf16[6144,1536]{1,0:T(8,128)(2,1)} %wq_hbm.1, ...), custom_call_target="tpu_custom_call" | custom-call | tf_op jit(solution)/shard_map/project/pallas_call | solution.py:502
  16.4 7.1 %attend.1 = (bf16[3,8,6144]{2,1,0:T(8,128)(2,1)S(1)}, f32[2304,128]{1,0:T(8,128)S(1)}, bf16[16,2048,128]{2,1,0:T(8,128)(2,1)S(1)}, bf16[16,2048,128]{2,1,0:T(8,1...) custom-call(s32[16]{0:T(128)} %lens_hbm.3, ...), custom_call_target="tpu_custom_call", output_to_operand_aliasing={{2}: (3, {}), {3}: (4, {})} | custom-call | tf_op jit(solution)/shard_map/attend/pallas_call | solution.py:535
  23.6 37.0 %output.1 = bf16[3,4,2,8,6144]{4,3,2,1,0:T(8,128)(2,1)S(1)} custom-call(s32[16]{0:T(128)} %lens_hbm.3, f32[2304,128]{1,0:T(8,128)S(1)} %get-tuple-element.13.q_rows, f32[2304,128]{1,0:T(8,128)S(1)} %get-tuple-element.17.o_first, bf16[16,2048,128]{2,1,0:T(8,128)(2,1)S(1)} %get-tuple-element.18.k_buf, bf16[16,2048,128]{2,1,0:T(8,128)(2,1)S(1)} %get-tuple-element.19.v_buf, ...), custom_call_target="tpu_custom_call" | custom-call | tf_op jit(solution)/shard_map/output/pallas_call | solution.py:558
  60.6 1.4 %emit.1 = bf16[3,64,6144]{2,1,0:T(8,128)(2,1)} custom-call(bf16[3,64,6144]{2,1,0:T(8,128)(2,1)S(1)} %bitcast.3), custom_call_target="tpu_custom_call" | custom-call | tf_op jit(solution)/shard_map/emit/pallas_call | solution.py:575

commit v4 on v3

--- a/solution.py
+++ b/solution.py
@@ -494,8 +494,8 @@
         mib = 2 ** 20
         dma = pltpu.SemaphoreType.DMA
 
-        q_chunks, block = 6, 32
-        n_first, n_early = 10, 14
+        q_chunks, block = 6, 64
+        n_first, n_early = 10, 13
         remote = dma((q_chunks, tp_size - 1))
         n_rows = n_steps * n_heads
         spread = VMEM((n_rows * local_rows, head_dim), F32)
@@ -550,13 +550,13 @@
             name="attend",
         )(in_hbm(seq_lens), q_rows, kv_rows, k_held, v_held, in_hbm(k_cache), in_hbm(v_cache))
 
-        o_chunks = 6
+        o_chunks = 4
         n_units = 2 * o_chunks
         width = d_model // n_units
         units = (n_units, n_steps * tp_size * set_rows, width)
         split = (n_steps, tp_size, 2, set_rows, d_model)
         y_held = pl.pallas_call(
-            functools.partial(output_kernel, (tp_size, o_chunks, 3, n_first)),
+            functools.partial(output_kernel, (tp_size, o_chunks, 2, n_first)),
             out_shape=VMEM(split, BF16),
             in_specs=[spec(pl.ANY)] + [spec(VMEM)] * 5 + [spec(pl.ANY)] * 3,
             out_specs=spec(VMEM),

time: 62.3 us -> 62.1 us (level)
  no operation moved by 1% of the time
where the time goes in v4:
time: 62.1 us; the launch traced here: 62.2 us
  Pallas kernels  61.4 us (99%)
  between operations  0.82 us (1%)
    pallas_call x1, Pallas kernels, local_block(): pl.pallas_call(functools.partial(output_kernel, (tp_size, o_chunks, 2, n_...  37.1 us
    pallas_call x1, Pallas kernels, local_block(): pl.pallas_call(functools.partial(project_kernel, (n_steps, group_rows, tp...  15.3 us
    pallas_call x1, Pallas kernels, local_block(): pl.pallas_call(functools.partial(attend_kernel, (n_first, n_early)), out_...  7.58 us
    pallas_call x1, Pallas kernels, local_block(): pl.pallas_call(emit_kernel, out_shape=jax.ShapeDtypeStruct(x_steps.shape,...  1.42 us

profile of v4, /device:TPU:0, one launch (start us, length us, event | category | flops | bytes accessed | tf_op | source)
XLA Modules:
  0.0 62.2 jit_solution(10516201235230986017)
XLA Ops:
  0.6 15.3 %project.1 = (f32[2304,128]{1,0:T(8,128)S(1)}, f32[2,3,16,128]{3,2,1,0:T(8,128)S(1)}, bf16[16,2048,128]{2,1,0:T(8,128)(2,1)S(1)}, bf16[16,2048,128]{2,1,0:T(8,128)(2,1)S(1)}) custom-call(bf16[192,6144]{1,0:T(8,128)(2,1)} %bitcast.4, bf16[6144]{0:T(1024)(128)(2,1)} %gain_hbm.1, bf16[6144]{0:T(1024)(128)(2,1)} %bias_hbm.1, bf16[6144,1536]{1,0:T(8,128)(2,1)} %wq_hbm.1, ...), custom_call_target="tpu_custom_call" | custom-call | tf_op jit(solution)/shard_map/project/pallas_call | solution.py:502
  15.9 7.6 %attend.1 = (bf16[3,8,6144]{2,1,0:T(8,128)(2,1)S(1)}, f32[2304,128]{1,0:T(8,128)S(1)}, bf16[16,2048,128]{2,1,0:T(8,128)(2,1)S(1)}, bf16[16,2048,128]{2,1,0:T(8,1...) custom-call(s32[16]{0:T(128)} %lens_hbm.3, ...), custom_call_target="tpu_custom_call", output_to_operand_aliasing={{2}: (3, {}), {3}: (4, {})} | custom-call | tf_op jit(solution)/shard_map/attend/pallas_call | solution.py:535
  23.5 37.1 %output.1 = bf16[3,4,2,8,6144]{4,3,2,1,0:T(8,128)(2,1)S(1)} custom-call(s32[16]{0:T(128)} %lens_hbm.3, f32[2304,128]{1,0:T(8,128)S(1)} %get-tuple-element.13.q_rows, f32[2304,128]{1,0:T(8,128)S(1)} %get-tuple-element.17.o_first, bf16[16,2048,128]{2,1,0:T(8,128)(2,1)S(1)} %get-tuple-element.18.k_buf, bf16[16,2048,128]{2,1,0:T(8,128)(2,1)S(1)} %get-tuple-element.19.v_buf, ...), custom_call_target="tpu_custom_call" | custom-call | tf_op jit(solution)/shard_map/output/pallas_call | solution.py:558
  60.7 1.4 %emit.1 = bf16[3,64,6144]{2,1,0:T(8,128)(2,1)} custom-call(bf16[3,64,6144]{2,1,0:T(8,128)(2,1)S(1)} %bitcast.3), custom_call_target="tpu_custom_call" | custom-call | tf_op jit(solution)/shard_map/emit/pallas_call | solution.py:575
